TPU v7x, 8 devices: a whole 2x2x1 slice. The times are simulated.
8 devices in a mesh: rep: 1 (over z), dp: 8 (over x, y, core).
Axes of the slice: x: 2, y: 2, z: 1, core: 2. Of those that a mesh axis runs over, the one named last changes fastest.
Arguments:
- x: bfloat16 [8, 2048, 1024], P(('rep', 'dp'))
- dy: bfloat16 [8, 2048, 1024], P(('rep', 'dp'))
- w_gate: bfloat16 [2, 1024, 6144], P(None, 'dp')
- w_up: bfloat16 [2, 1024, 6144], P(None, 'dp')
- w_down: bfloat16 [2, 6144, 1024], P(None, 'dp')
Outputs:
- output 1: bfloat16 [8, 2048, 1024], P(('rep', 'dp'))
- output 2: bfloat16 [2, 1024, 6144], P('rep', 'dp')
- output 3: bfloat16 [2, 1024, 6144], P('rep', 'dp')
- output 4: bfloat16 [2, 6144, 1024], P('rep', 'dp')
All inputs are finite; a program needn't handle non-finite values.
Results may differ from a plain program's by a relative error of at most 0.018.
Values are sent between devices in bfloat16 or wider.
A program may use at most 2 GiB of HBM per device.

v0:
```python
import jax
import jax.numpy as jnp
from jax import lax

NAMES = ("w_gate", "w_up", "w_down")


def matmul(a, w):
    return jnp.dot(a, w, preferred_element_type=jnp.float32).astype(jnp.bfloat16)


def normed(h):
    wide = h.astype(jnp.float32)
    scale = lax.rsqrt(jnp.mean(wide**2, -1, keepdims=True) + 1e-6)
    return (wide * scale).astype(jnp.bfloat16)


def layer(h, w):
    a = normed(h)
    gate = jnp.dot(a, w["w_gate"], preferred_element_type=jnp.float32)
    up = jnp.dot(a, w["w_up"], preferred_element_type=jnp.float32)
    return h + matmul((jax.nn.silu(gate) * up).astype(jnp.bfloat16), w["w_down"])


def stack(weights, h):
    for number in range(weights["w_gate"].shape[0]):
        h = layer(h, {name: w[number] for name, w in weights.items()})
    return h


def solution(mesh):
    groups = mesh.shape["rep"]

    def step(x, dy, *weights):
        shape = x.shape
        x, dy = (t.reshape(groups, -1, *t.shape[1:]) for t in (x, dy))

        def of_a_group(x, dy):
            _, back = jax.vjp(stack, dict(zip(NAMES, weights, strict=True)), x)
            by_weights, by_x = back(dy)
            return (by_x, *(by_weights[name] for name in NAMES))

        by_x, *by_weights = jax.vmap(of_a_group)(x, dy)
        return (by_x.reshape(shape), *(t.reshape(-1, *t.shape[2:]) for t in by_weights))

    return step
```

profile of v0, /device:TPU:0, one launch (start us, length us, event | category | flops | bytes accessed | tf_op | source)
XLA Modules:
  0.0 1450.0 jit_solution(3159848270050209754)
XLA Ops:
  35.9 44.8 %all-gather.30.cloned.1.call-done = bf16[1,1024,6144]{2,1,0:T(8,128)(2,1)} async-done(((bf16[1,128,6144]{2,1,0:T(8,128)(2,1)}), bf16[1,1024,6144]{2,1,0:T(8,128)(2,1)}) %all-gather.30.cloned.1.call-update) | async-done | bytes 12582928 | tf_op jit(solution)/vmap(jvp())/squeeze | solution.py:27
  80.7 36.2 %fusion.48 = f32[2048,6144]{1,0:T(8,128)} fusion(bf16[1,1024,6144]{2,1,0:T(8,128)(2,1)} %all-gather.30.cloned.1.call-done, bf16[1,2048,1024]{1,2,0:T(8,128)(2,1)} %copy.1, f32[2048]{0:T(1024)S(1)} %bitcast.274), kind=kOutput, calls=%fused_computation.67 | convolution fusion | flops 25776095232 | bytes 67117056 | tf_op jit(solution)/vmap(jvp())/dot_general | solution.py:20
  116.9 32.7 %all-gather.32.cloned.1.call-done = bf16[1,1024,6144]{2,1,0:T(8,128)(2,1)} async-done(((bf16[1,128,6144]{2,1,0:T(8,128)(2,1)}), bf16[1,1024,6144]{2,1,0:T(8,128)(2,1)}) %all-gather.32.cloned.1.call-update) | async-done | bytes 12582928 | tf_op jit(solution)/vmap(jvp())/squeeze | solution.py:27
  149.6 35.6 %fusion.44 = f32[2048,6144]{1,0:T(8,128)} fusion(bf16[1,1024,6144]{2,1,0:T(8,128)(2,1)} %all-gather.32.cloned.1.call-done, bf16[1,2048,1024]{1,2,0:T(8,128)(2,1)} %copy.1, f32[2048]{0:T(1024)S(1)} %bitcast.275), kind=kOutput, calls=%fused_computation.63 | convolution fusion | flops 25776095232 | bytes 67117056 | tf_op jit(solution)/vmap(jvp())/dot_general | solution.py:21
  185.2 40.8 %fusion.24 = bf16[2048,6144]{1,0:T(8,128)(2,1)} fusion(f32[2048,6144]{1,0:T(8,128)} %fusion.44, f32[2048,6144]{1,0:T(8,128)} %fusion.48), kind=kLoop, calls=%fused_computation.34 | loop fusion | flops 75497472 | bytes 125829120
  226.0 34.4 %convolution_convert_fusion.1 = bf16[2048,6144]{1,0:T(8,128)(2,1)} fusion(bf16[1,6144,1024]{2,1,0:T(8,128)(2,1)} %all-gather.38.cloned.1.call-done, bf16[1,2048,1024]{2,1,0:T(8,128)(2,1)} %param), kind=kOutput, calls=%fused_computation.42 | convolution fusion | flops 25782386688 | bytes 41943040 | tf_op jit(solution)/vmap(transpose(jvp()))/dot_general | solution.py:9
  286.0 46.7 %fusion.57 = (f32[2048]{0:T(1024)S(1)}, bf16[1,2048,1024]{1,2,0:T(8,128)(2,1)}) fusion(bf16[1,2048,1024]{1,2,0:T(8,128)(2,1)} %copy.1, bf16[2048,6144]{1,0:T(8,128)(2,1)} %fusion.24, bf16[1,6144,1024]{2,1,0:T(8,128)(2,1)} %all-gather.34.cloned.1.call-done), kind=kOutput, calls=%fused_computation.78 | convolution fusion | flops 25780287488 | bytes 46145536 | tf_op jit(solution)/vmap(jvp())/dot_general | solution.py:9
  354.7 36.1 %fusion.38 = f32[2048,6144]{1,0:T(8,128)} fusion(bf16[1,1024,6144]{2,1,0:T(8,128)(2,1)} %all-gather.36.cloned.1.call-done, bf16[1,2048,1024]{1,2,0:T(8,128)(2,1)} %get-tuple-element.11, f32[2048]{0:T(1024)S(1)} %bitcast.279), kind=kOutput, calls=%fused_computation.57 | convolution fusion | flops 25776095232 | bytes 67117056 | tf_op jit(solution)/vmap(jvp())/dot_general | solution.py:20
  390.8 43.8 %fusion.20 = f32[6144,1024]{1,0:T(8,128)} fusion(bf16[2048,6144]{1,0:T(8,128)(2,1)} %convolution_convert_fusion.1, f32[2048,6144]{1,0:T(8,128)} %fusion.38, bf16[1,2048,1024]{1,2,0:T(8,128)(2,1)} %get-tuple-element.11, f32[2048]{0:T(1024)S(1)} %bitcast.280), kind=kOutput, calls=%fused_computation.32 | convolution fusion | flops 25851592704 | bytes 104865792 | tf_op jit(solution)/vmap(transpose(jvp()))/dot_general | solution.py:21
  434.7 37.9 %fusion.32 = f32[2048,6144]{1,0:T(8,128)} fusion(bf16[1,1024,6144]{2,1,0:T(8,128)(2,1)} %all-gather.40.cloned.1.call-done, bf16[1,2048,1024]{1,2,0:T(8,128)(2,1)} %get-tuple-element.11, f32[2048]{0:T(1024)S(1)} %bitcast.281), kind=kOutput, calls=%fused_computation.51 | convolution fusion | flops 25776095232 | bytes 67117056 | tf_op jit(solution)/vmap(jvp())/dot_general | solution.py:21
  472.6 52.4 %fusion.4 = bf16[2048,6144]{1,0:T(8,128)(2,1)} fusion(f32[2048,6144]{1,0:T(8,128)} %fusion.38, f32[2048,6144]{1,0:T(8,128)} %fusion.32, bf16[2048,6144]{1,0:T(8,128)(2,1)} %convolution_convert_fusion.1), kind=kLoop, calls=%fused_computation.10 | loop fusion | flops 150994944 | bytes 150994944
  525.0 34.9 %fusion.36 = bf16[2048,1024]{0,1:T(8,128)(2,1)} fusion(bf16[2048,6144]{1,0:T(8,128)(2,1)} %fusion.4, bf16[1,1024,6144]{2,1,0:T(8,128)(2,1)} %all-gather.36.cloned.1.call-done), kind=kOutput, calls=%fused_computation.55 | convolution fusion | flops 25769803776 | bytes 41943040 | tf_op jit(solution)/vmap(transpose(jvp()))/dot_general | solution.py:20
  560.0 41.9 %fusion.59 = (f32[2048]{0:T(1024)S(1)}, bf16[2048,1024]{0,1:T(8,128)(2,1)}) fusion(bf16[1,2048,1024]{1,2,0:T(8,128)(2,1)S(1)} %copy-done.4, bf16[2048,1024]{0,1:T(8,128)(2,1)} %fusion.36, bf16[1,1024,6144]{2,1,0:T(8,128)(2,1)} %all-gather.40.cloned.1.call-done, bf16[2048,6144]{1,0:T(8,128)(2,1)} %convolution_convert_fusion.1, f32[2048,6144]{1,0:T(8,128)} %fusion.38), kind=kOutput, calls=%fused_computation.80 | convolution fusion | flops 25857882112 | bytes 100671488 | tf_op jit(solution)/vmap(transpose(jvp()))/dot_general | solution.py:21
  608.1 33.9 %convolution_convert_fusion = bf16[2048,6144]{1,0:T(8,128)(2,1)} fusion(bf16[1,6144,1024]{2,1,0:T(8,128)(2,1)} %all-gather.34.cloned.1.call-done, bf16[1,2048,1024]{1,2,0:T(8,128)(2,1)} %fusion.63), kind=kOutput, calls=%fused_computation.41 | convolution fusion | flops 25782386688 | bytes 41943040 | tf_op jit(solution)/vmap(transpose(jvp()))/dot_general | solution.py:9
  642.0 43.6 %fusion.16 = f32[6144,1024]{1,0:T(8,128)} fusion(bf16[2048,6144]{1,0:T(8,128)(2,1)} %convolution_convert_fusion, f32[2048,6144]{1,0:T(8,128)} %fusion.48, bf16[1,2048,1024]{1,2,0:T(8,128)(2,1)} %copy.1, f32[2048]{0:T(1024)S(1)} %bitcast.276), kind=kOutput, calls=%fused_computation.30 | convolution fusion | flops 25851592704 | bytes 104865792 | tf_op jit(solution)/vmap(transpose(jvp()))/dot_general | solution.py:21
  686.2 34.1 %fusion.85 = f32[6144,1024]{1,0:T(8,128)} fusion(bf16[2048,6144]{1,0:T(8,128)(2,1)} %fusion.4, bf16[1,2048,1024]{1,2,0:T(8,128)(2,1)} %get-tuple-element.11, f32[2048]{0:T(1024)S(1)} %bitcast.283), kind=kOutput, calls=%fused_computation.97 | convolution fusion | flops 25776095232 | bytes 54534144 | tf_op jit(solution)/vmap(transpose(jvp()))/dot_general | solution.py:20
  720.5 54.1 %fusion.7 = bf16[2048,6144]{1,0:T(8,128)(2,1)} fusion(f32[2048,6144]{1,0:T(8,128)} %fusion.48, f32[2048,6144]{1,0:T(8,128)} %fusion.44, bf16[2048,6144]{1,0:T(8,128)(2,1)} %convolution_convert_fusion), kind=kLoop, calls=%fused_computation.13 | loop fusion | flops 150994944 | bytes 150994944
  806.2 33.3 %fusion.64 = f32[1024,6144]{0,1:T(8,128)} fusion(bf16[2048,6144]{1,0:T(8,128)(2,1)} %fusion.24, bf16[1,2048,1024]{1,2,0:T(8,128)(2,1)} %fusion.63), kind=kOutput, calls=%fused_computation.85 | convolution fusion | flops 25769803776 | bytes 54525952 | tf_op jit(solution)/vmap(transpose(jvp()))/dot_general | solution.py:9
  839.5 56.5 %fusion.26 = f32[6144,1024]{1,0:T(8,128)} fusion(f32[2048,6144]{1,0:T(8,128)} %fusion.32, f32[2048,6144]{1,0:T(8,128)} %fusion.38, bf16[1,2048,1024]{2,1,0:T(8,128)(2,1)} %param), kind=kOutput, calls=%fused_computation.36 | convolution fusion | flops 25845301248 | bytes 130023424 | tf_op jit(solution)/vmap(transpose(jvp()))/dot_general | solution.py:9
  896.1 34.8 %fusion.46 = bf16[2048,1024]{0,1:T(8,128)(2,1)} fusion(bf16[2048,6144]{1,0:T(8,128)(2,1)} %fusion.7, bf16[1,1024,6144]{2,1,0:T(8,128)(2,1)} %all-gather.30.cloned.1.call-done), kind=kOutput, calls=%fused_computation.65 | convolution fusion | flops 25769803776 | bytes 41943040 | tf_op jit(solution)/vmap(transpose(jvp()))/dot_general | solution.py:20
  931.0 43.8 %fusion.56 = (f32[2048]{0:T(1024)S(1)}, bf16[2048,1024]{0,1:T(8,128)(2,1)}) fusion(bf16[1,2048,1024]{1,2,0:T(8,128)(2,1)S(1)} %copy-done.1, bf16[2048,1024]{0,1:T(8,128)(2,1)} %fusion.46, bf16[1,1024,6144]{2,1,0:T(8,128)(2,1)} %all-gather.32.cloned.1.call-done, bf16[2048,6144]{1,0:T(8,128)(2,1)} %convolution_convert_fusion, f32[2048,6144]{1,0:T(8,128)} %fusion.48), kind=kOutput, calls=%fused_computation.77 | convolution fusion | flops 25857882112 | bytes 100671488 | tf_op jit(solution)/vmap(transpose(jvp()))/dot_general | solution.py:21
  1001.8 133.9 %reduce-scatter.21.cloned.1.call-done = f32[6144,128]{1,0:T(8,128)} async-done(((f32[6144,1024]{1,0:T(8,128)}), f32[6144,128]{1,0:T(8,128)}) %reduce-scatter.21.cloned.1.call-update) | async-done | bytes 3145744
  1142.2 145.1 %reduce-scatter.29.cloned.1.call-done = f32[1024,768]{0,1:T(8,128)} async-done(((f32[1024,6144]{0,1:T(8,128)}), f32[1024,768]{0,1:T(8,128)}) %reduce-scatter.29.cloned.1.call-update) | async-done | bytes 3145744
  1289.5 149.3 %reduce-scatter.27.cloned.1.call-done = f32[768,1024]{1,0:T(8,128)} async-done(((f32[6144,1024]{1,0:T(8,128)}), f32[768,1024]{1,0:T(8,128)}) %reduce-scatter.27.cloned.1.call-update) | async-done | bytes 3145744
  (90 shorter events, 154.5 us)
Async XLA Ops:
  7.2 73.5 %all-gather.30.cloned.1.call-start = ((), (), s32[]{:S(2)}) async-start(), calls=%async_computation.6 | async-start | bytes 14155776 | tf_op jit(solution)/vmap(jvp())/squeeze | solution.py:27
  11.3 138.3 %all-gather.32.cloned.1.call-start = ((), (), s32[]{:S(2)}) async-start(), calls=%async_computation.7 | async-start | bytes 14155776 | tf_op jit(solution)/vmap(jvp())/squeeze | solution.py:27
  15.3 210.7 %all-gather.38.cloned.1.call-start = ((), (), s32[]{:S(2)}) async-start(), calls=%async_computation.10 | async-start | bytes 14155776 | tf_op jit(solution)/vmap(jvp())/squeeze | solution.py:27
  17.3 268.7 %all-gather.34.cloned.1.call-start = ((), (), s32[]{:S(2)}) async-start(), calls=%async_computation.8 | async-start | bytes 14155776 | tf_op jit(solution)/vmap(jvp())/squeeze | solution.py:27
  17.9 336.8 %all-gather.36.cloned.1.call-start = ((), (), s32[]{:S(2)}) async-start(), calls=%async_computation.9 | async-start | bytes 14155776 | tf_op jit(solution)/vmap(jvp())/squeeze | solution.py:27
  18.5 416.2 %all-gather.40.cloned.1.call-start = ((), (), s32[]{:S(2)}) async-start(), calls=%async_computation.11 | async-start | bytes 14155776 | tf_op jit(solution)/vmap(jvp())/squeeze | solution.py:27
  19.0 968.3 %reduce-scatter.23.cloned.1.call-start = ((), (), s32[]{:S(2)}) async-start(), calls=%async_computation.14 | async-start | bytes 28311552
  29.5 120.1 %copy-start.10 = (f32[1,2048]{1,0:T(1,128)}, f32[1,2048]{1,0:T(1,128)S(1)}, u32[]{:S(2)}) copy-start(f32[1,2048]{1,0:T(1,128)S(1)} %rsqrt.22) | copy-start | bytes 24580
  333.4 101.3 %copy-start.13 = (f32[1,2048]{1,0:T(1,128)}, f32[1,2048]{1,0:T(1,128)S(1)}, u32[]{:S(2)}) copy-start(f32[1,2048]{1,0:T(1,128)S(1)} %rsqrt.23) | copy-start | bytes 24580
  434.6 555.9 %reduce-scatter.25.cloned.1.call-start = ((), (), s32[]{:S(2)}) async-start(), calls=%async_computation.15 | async-start | bytes 28311552
  525.0 34.9 %copy-start.4 = (bf16[1,2048,1024]{1,2,0:T(8,128)(2,1)S(1)}, bf16[1,2048,1024]{1,2,0:T(8,128)(2,1)}, u32[]{:S(2)}) copy-start(bf16[1,2048,1024]{1,2,0:T(8,128)(2,1)} %get-tuple-element.11) | copy-start | bytes 12582916
  560.0 42.0 %copy-start.9 = (f32[2048]{0:T(1024)S(1)}, f32[2048]{0:T(1024)}, u32[]{:S(2)}) copy-start(f32[2048]{0:T(1024)} %copy-done.8) | copy-start | bytes 24580
  560.0 42.0 %copy-start.3 = (bf16[1,2048,1024]{1,2,0:T(8,128)(2,1)S(1)}, bf16[1,2048,1024]{1,2,0:T(8,128)(2,1)}, u32[]{:S(2)}) copy-start(bf16[1,2048,1024]{1,2,0:T(8,128)(2,1)} %copy.2) | copy-start | bytes 12582916
  560.0 42.0 %copy-start.14 = (f32[1,2048]{1,0:T(1,128)S(1)}, f32[1,2048]{1,0:T(1,128)}, u32[]{:S(2)}) copy-start(f32[1,2048]{1,0:T(1,128)} %copy-done.13) | copy-start | bytes 24580
  608.1 33.9 %copy-start.11 = (f32[1,2048]{1,0:T(1,128)S(1)}, f32[1,2048]{1,0:T(1,128)}, u32[]{:S(2)}) copy-start(f32[1,2048]{1,0:T(1,128)} %copy-done.10) | copy-start | bytes 24580
  685.6 312.4 %reduce-scatter.19.cloned.1.call-start = ((), (), s32[]{:S(2)}) async-start(), calls=%async_computation.12 | async-start | bytes 28311552
  720.4 415.4 %reduce-scatter.21.cloned.1.call-start = ((), (), s32[]{:S(2)}) async-start(), calls=%async_computation.13 | async-start | bytes 28311552
  720.5 54.1 %copy-start = (bf16[1,2048,1024]{1,2,0:T(8,128)(2,1)S(1)}, bf16[1,2048,1024]{1,2,0:T(8,128)(2,1)}, u32[]{:S(2)}) copy-start(bf16[1,2048,1024]{1,2,0:T(8,128)(2,1)} %copy.1) | copy-start | bytes 12582916
  806.1 481.2 %reduce-scatter.29.cloned.1.call-start = ((), (), s32[]{:S(2)}) async-start(), calls=%async_computation.17 | async-start | bytes 28311552
  839.5 599.3 %reduce-scatter.27.cloned.1.call-start = ((), (), s32[]{:S(2)}) async-start(), calls=%async_computation.16 | async-start | bytes 28311552
  896.1 34.9 %copy-start.1 = (bf16[1,2048,1024]{1,2,0:T(8,128)(2,1)S(1)}, bf16[1,2048,1024]{1,2,0:T(8,128)(2,1)}, u32[]{:S(2)}) copy-start(bf16[1,2048,1024]{1,2,0:T(8,128)(2,1)} %copy.1) | copy-start | bytes 12582916
  930.9 43.8 %copy-start.7 = (f32[2048]{0:T(1024)S(1)}, f32[2048]{0:T(1024)}, u32[]{:S(2)}) copy-start(f32[2048]{0:T(1024)} %copy-done.6) | copy-start | bytes 24580
  930.9 43.8 %copy-start.2 = (bf16[1,2048,1024]{1,2,0:T(8,128)(2,1)S(1)}, bf16[1,2048,1024]{1,2,0:T(8,128)(2,1)}, u32[]{:S(2)}) copy-start(bf16[1,2048,1024]{1,2,0:T(8,128)(2,1)} %fusion.63) | copy-start | bytes 12582916
  931.0 43.8 %copy-start.12 = (f32[1,2048]{1,0:T(1,128)S(1)}, f32[1,2048]{1,0:T(1,128)}, u32[]{:S(2)}) copy-start(f32[1,2048]{1,0:T(1,128)} %copy-done.10) | copy-start | bytes 24580
  (4 other events, 10.0 us)
Sparse Core Ops, SparseCore 0:
  11.4 69.2 all-gather.29
  83.1 66.4 all-gather.31
  151.4 66.4 all-gather.37
  219.5 66.4 all-gather.33
  288.2 66.4 all-gather.35
  357.0 66.4 all-gather.39
  434.7 148.0 reduce-scatter.22
  685.7 147.7 reduce-scatter.24
  837.0 147.6 reduce-scatter.18
  988.1 147.6 reduce-scatter.20
  1139.3 147.9 reduce-scatter.28
  1290.7 147.9 reduce-scatter.26
where the time goes:
time: 1460 us; the launch traced here: 1450 us
  matrix products  659 us (45%)
  waiting for transfers between devices  554 us (38%)
  other arithmetic  184 us (13%)
  local copies, waits for them, and re-layouts  36.9 us (3%)
  between operations  14.8 us (1%)
    unnamed x18, waiting for transfers between devices  430 us
    dot_general x6, matrix products, layer(): up = jnp.dot(a, w['w_up'], preferred_element_type=jnp.float32)  247 us
    dot_general x6, matrix products, layer(): gate = jnp.dot(a, w['w_gate'], preferred_element_type=jnp.float32)  208 us
    dot_general x5, matrix products, matmul(): jnp.dot(a, w, preferred_element_type=jnp.float32).astype(jnp.bfloat16)  205 us
    unnamed x3, other arithmetic  147 us
    squeeze x6, waiting for transfers between devices, stack(): h = layer(h, {name: w[number] for name, w in weights.items()})  124 us
  transfers between devices with their start and end apart: 12, of which 7 were waited for; matrix products, arithmetic and copies ran while one was open for 60% of the time, Pallas kernels for 0%

commit v1 on v0

v1 whole, which is shorter than its diff:
```python
import functools

import jax
import jax.numpy as jnp
from jax import lax
from jax.experimental import pallas as pl
from jax.experimental.pallas import tpu as pltpu
from jax.sharding import PartitionSpec as P


F32, BF16 = jnp.float32, jnp.bfloat16
NN = (((1,), (0,)), ((), ()))
NT = (((1,), (1,)), ((), ()))
TN = (((0,), (0,)), ((), ()))
ONE = pl.Buffered(1)

NEXT = (1, 3, 0, 2)
PREV = (2, 0, 3, 1)
RIGHT = [(2 * c + k, 2 * NEXT[c] + k) for c in range(4) for k in range(2)]
LEFT = [(2 * c + k, 2 * PREV[c] + k) for c in range(4) for k in range(2)]
ACROSS = [(d, d ^ 1) for d in range(8)]
ORDER = [[2 * chip + core for core in (1 - k, k) for chip in (3 - c, PREV[c], NEXT[c], c)] for c in range(4) for k in range(2)]


def dot(a, b, dims):
    return lax.dot_general(a, b, dims, preferred_element_type=F32)


def shape(dims, dtype):
    return jax.ShapeDtypeStruct(dims, dtype)


def place():
    me = lax.axis_index("dp")
    x, y, k = me // 4, (me // 2) % 2, me % 2
    return me, (2 * y + 1 - x) * 2 + k, (2 * (1 - y) + x) * 2 + k, me + 1 - 2 * k


def gather_copies(own, whole, send, recv):
    me, nxt, prv, other = place()
    n = whole.shape[0] // 8
    half = n // 2
    rows = lambda d, start=0, size=n: whole.at[pl.ds(pl.multiple_of(d * n + start, 8), size)]
    opp = 6 - me + 2 * (me % 2)

    def copy(i, src, dst, to):
        return pltpu.make_async_remote_copy(
            src_ref=src, dst_ref=dst, send_sem=send.at[i], recv_sem=recv.at[i], device_id={"dp": to}, device_id_type=pl.DeviceIdType.MESH
        )

    return [
        copy(0, own, rows(me), nxt),
        copy(1, own, rows(me), prv),
        copy(2, own, rows(me), other),
        copy(3, rows(prv, 0, half), rows(prv, 0, half), nxt),
        copy(4, rows(nxt, half, half), rows(nxt, half, half), prv),
        copy(5, rows(prv), rows(prv), other),
        copy(6, rows(nxt), rows(nxt), other),
        copy(7, rows(opp), rows(opp), other),
        pltpu.make_async_copy(own, rows(me), send.at[8]),
    ]


class Gather:
    def __init__(self, number, units, ticks):
        self.number, self.units, self.ticks = number, units, ticks


def call(body, grid, ins, outs, flops, nbytes, prefetch=0, gather=None, kept=(), vmem=62 * 2**20):
    n_in, n_out, n_kept = prefetch + len(ins), len(outs), len(kept)
    hbm = pl.BlockSpec(memory_space=pl.ANY)
    units = gather.units if gather else []
    specs, shapes, scratch, whole = list(ins) + [hbm] * n_kept, [o for _, o in outs], [], body
    if gather:
        steps = grid[0]

        def whole(*refs):
            owns = [part(r) for r, (_, part, _) in zip(refs[n_in + n_kept:], units)]
            results = refs[n_in + n_kept + len(units):]
            wholes, send, recv = results[n_out:n_out + len(units)], results[-2], results[-1]
            copies = [gather_copies(o, w, send.at[u], recv.at[u]) for u, (o, w) in enumerate(zip(owns, wholes))]
            step = pl.program_id(0)

            def first():
                barrier = pltpu.get_barrier_semaphore()
                for d in place()[1:]:
                    pl.semaphore_signal(barrier, inc=1, device_id={"dp": d}, device_id_type=pl.DeviceIdType.MESH)
                pl.semaphore_wait(barrier, 3)
                for c in copies:
                    for i in (0, 1, 2, 8):
                        c[i].start()

            def second(c):
                c[0].wait_recv()
                c[1].wait_recv()
                for i in (3, 4, 5, 6):
                    c[i].start()

            def third(c):
                c[3].wait_recv()
                c[4].wait_recv()
                c[7].start()

            def last():
                for c in copies:
                    for i in (2, 5, 6, 7):
                        c[i].wait_recv()
                    for i in range(8):
                        c[i].wait_send()
                    c[8].wait()

            pl.when(step == 0)(first)
            for c, (two, three) in zip(copies, gather.ticks):
                pl.when(step == two)(functools.partial(second, c))
                if three < steps:
                    pl.when(step == three)(functools.partial(third, c))
            body(*refs[:n_in], *results[:n_out])

            @pl.when(step == steps - 1)
            def _():
                for c, (_, three) in zip(copies, gather.ticks):
                    if three >= steps:
                        third(c)
                last()

        specs += [hbm] * len(units)
        outs = list(outs) + [(hbm, shape((8 * n, w.shape[-1] if cols is None else cols), BF16)) for w, _, (n, cols) in units]
        shapes = [o for _, o in outs]
        scratch = [pltpu.SemaphoreType.DMA((len(units), 9)), pltpu.SemaphoreType.DMA((len(units), 8))]
        extra = dict(collective_id=gather.number, has_side_effects=True)
    else:
        extra = {}
        if kept:
            def whole(*refs):
                body(*refs[:n_in], *refs[n_in + n_kept:])
    made = pl.pallas_call(
        whole,
        grid_spec=pltpu.PrefetchScalarGridSpec(
            num_scalar_prefetch=prefetch, grid=grid, in_specs=specs, out_specs=[s for s, _ in outs], scratch_shapes=scratch
        ),
        out_shape=shapes,
        input_output_aliases={n_in + i: i for i in range(n_kept)},
        cost_estimate=pl.CostEstimate(flops=flops, bytes_accessed=nbytes, transcendentals=0),
        compiler_params=pltpu.CompilerParams(vmem_limit_bytes=vmem, dimension_semantics=("arbitrary",) * len(grid), **extra),
    )

    def run(*args):
        got = made(*args, *kept, *(u[0] for u in units))
        return got[0] if len(outs) == 1 else got

    return run


def pieces(rows, cols):
    return [(rows // 8, cols)] * 6 + [(rows // 4, cols)]


def by_rows(at, d, half, got=None, bn=1024):
    T, N = d.shape
    rows = at.shape[0] // 2
    h = rows // 8

    def theirs(a_ref, d_ref, o_ref):
        o_ref[...] = dot(a_ref[...], d_ref[...], NN).astype(BF16)

    def mine(a_ref, d_ref, got_ref, *outs):
        t = (dot(a_ref[...], d_ref[...], NN) + got_ref[...].astype(F32)).astype(BF16)
        for i in range(6):
            outs[i][...] = t[i * h:(i + 1) * h, :]
        outs[6][...] = t[6 * h:, :]

    col = lambda j: (0, j)
    ins = [pl.BlockSpec((rows, T), lambda j: (half, 0), pipeline_mode=ONE), pl.BlockSpec((T, bn), col)]
    args, results = [at, d], [(rows, N)]
    if got is not None:
        ins.append(pl.BlockSpec((rows, bn), col))
        args.append(got)
        results = pieces(rows, N)
    outs = [(pl.BlockSpec((r, bn), col), shape((r, N), BF16)) for r, _ in results]
    return call(theirs if got is None else mine, (N // bn,), ins, outs, 2 * rows * T * N, T * N * 2)(*args)


def by_blocks(order, p, d, got=None, parts=1):
    T, D = d.shape
    n, bm = order.shape[0], p.shape[1] // 8
    width, h = bm // parts, bm // 2

    def theirs(order_ref, *refs):
        for c in range(parts):
            refs[-1][c * width:(c + 1) * width, :] = dot(refs[c][...], refs[parts][...], TN).astype(BF16)

    def mine(order_ref, *refs):
        outs, step = refs[parts + 2:], pl.program_id(0)
        for c in range(parts):
            r = slice(c * width, (c + 1) * width)
            t = dot(refs[c][...], refs[parts][...], TN)
            refs[parts + 1][r, :] = (t + refs[parts + 1][r, :].astype(F32)).astype(BF16)
        for i in range(3):
            @pl.when(step == i)
            def _():
                outs[2 * i][...] = refs[parts + 1][:h, :]
                outs[2 * i + 1][...] = refs[parts + 1][h:, :]

        @pl.when(step == 3)
        def _():
            outs[6][...] = refs[parts + 1][...]

    ins = [pl.BlockSpec((T, width), functools.partial(lambda c, i, o: (0, c * 8 + o[i]), c)) for c in range(parts)]
    ins.append(pl.BlockSpec((T, D), lambda i, o: (0, 0), pipeline_mode=ONE))
    args = [order, *[p] * parts, d]
    block = pl.BlockSpec((bm, D), lambda i, o: (i, 0))
    outs = [(block, shape((n * bm, D), BF16))]
    if got is not None:
        ins.append(block)
        args.append(got)
        outs = [(pl.BlockSpec(s, lambda i, o: (0, 0)), shape(s, BF16)) for s in pieces(n * bm, D)]
    return call(theirs if got is None else mine, (n,), ins, outs, 2 * n * bm * T * D, T * n * bm * 2, prefetch=1)(*args)


def sent(t, pairs):
    return lax.ppermute(t, "dp", pairs)


def gateup(a, wg, wu, gather, bn=256, bm=512):
    T, D = a.shape
    N = wg.shape[1]

    def body(a_ref, wg_ref, wu_ref, p_ref, u_ref, g_ref):
        for i in range(T // bm):
            r = slice(i * bm, (i + 1) * bm)
            gate = dot(a_ref[r, :], wg_ref[...], NN)
            up = dot(a_ref[r, :], wu_ref[...], NN)
            s = jax.nn.sigmoid(gate)
            silu = gate * s
            p_ref[r, :] = (silu * up).astype(BF16)
            u_ref[r, :] = silu
            g_ref[r, :] = up * (0.5 * (s + silu * (1 - s)))

    col = lambda j: (0, j)
    w, o = pl.BlockSpec((D, bn), col), pl.BlockSpec((T, bn), col)
    return call(
        body, (N // bn,), [pl.BlockSpec((T, D), lambda j: (0, 0), pipeline_mode=ONE), w, w],
        [(o, shape((T, N), BF16)), (o, shape((T, N), F32)), (o, shape((T, N), F32))], 4 * T * D * N, T * N * 10, gather=gather,
    )(a, wg, wu)


def dproduct(dy, wd, by_u, by_g, bm=256, bn=1024):
    T, D = dy.shape
    N = wd.shape[0]

    def body(d_ref, w_ref, u_ref, g_ref, du_ref, dg_ref):
        for i in range(N // bn):
            r = slice(i * bn, (i + 1) * bn)
            dp = dot(d_ref[...], w_ref[r, :], NT).astype(BF16).astype(F32)
            du_ref[:, r] = (dp * u_ref[:, r]).astype(BF16)
            dg_ref[:, r] = (dp * g_ref[:, r] * 2.0).astype(BF16)

    row = lambda j: (j, 0)
    o = pl.BlockSpec((bm, N), row)
    return call(
        body, (T // bm,), [pl.BlockSpec((bm, D), row), pl.BlockSpec((N, D), lambda j: (0, 0), pipeline_mode=ONE), o, o],
        [(o, shape((T, N), BF16)), (o, shape((T, N), BF16))], 2 * T * D * N, T * N * 12,
    )(dy, wd, by_u, by_g)


def both(a, dy, wg, wu, wd, start, gather, kept, bn=256, bm=256):
    T, D = a.shape
    N = wg.shape[1]

    def body(a_ref, d_ref, wg_ref, wu_ref, wd_ref, p_ref, du_ref, dg_ref):
        for i in range(T // bm):
            r = slice(i * bm, (i + 1) * bm)
            gate = dot(a_ref[r, :], wg_ref[...], NN)
            up = dot(a_ref[r, :], wu_ref[...], NN)
            dp = dot(d_ref[r, :], wd_ref[...], NT).astype(BF16).astype(F32)
            s = jax.nn.sigmoid(gate)
            silu = gate * s
            p_ref[r, :] = (silu * up).astype(BF16)
            du_ref[r, :] = (dp * silu).astype(BF16)
            dg_ref[r, :] = (dp * up * (s + silu * (1 - s))).astype(BF16)

    col = lambda j: (0, j)
    full = pl.BlockSpec((T, D), lambda j: (0, 0), pipeline_mode=ONE)
    w, o = pl.BlockSpec((D, bn), col), pl.BlockSpec((T, bn), lambda j: (0, start // bn + j))
    return call(
        body, (N // bn,), [full, full, w, w, pl.BlockSpec((bn, D), lambda j: (start // bn + j, 0))],
        [(o, shape((T, wd.shape[0]), BF16))] * 3, 6 * T * D * N, T * N * 6, gather=gather, kept=kept,
    )(a, dy, wg, wu, wd)


def dnormed(dg, wgs, du, wus, h, g, start, steps, kept, bm=256):
    n = len(wgs)
    T, K = dg.shape
    D = wgs[0].shape[0]

    def product(d_ref, refs):
        total, at = None, 0
        for r in refs:
            t = dot(d_ref[:, at:at + r.shape[1]], r[...], NT)
            total, at = t if total is None else total + t, at + r.shape[1]
        return total.astype(BF16)

    def body(dg_ref, du_ref, *refs):
        h_ref, g_ref, o_ref = refs[2 * n:]
        da = (product(dg_ref, refs[:n]) + product(du_ref, refs[n:2 * n])).astype(F32)
        wide = h_ref[...].astype(F32)
        scale = lax.rsqrt(jnp.mean(wide**2, -1, keepdims=True) + 1e-6)
        inner = jnp.mean(da * wide, -1, keepdims=True)
        o_ref[...] = g_ref[...] + (da * scale - wide * (scale * scale * scale * inner)).astype(BF16)

    row = lambda i: (start + i, 0)
    full = [pl.BlockSpec(w.shape, lambda i: (0, 0), pipeline_mode=ONE) for w in (*wgs, *wus)]
    d, o = pl.BlockSpec((bm, K), row), pl.BlockSpec((bm, D), row)
    return call(
        body, (steps,), [d, d, *full, o, o], [(o, shape((T, D), BF16))], 4 * steps * bm * K * D, steps * bm * K * 4, kept=kept,
    )(dg, du, *wgs, *wus, h, g)


def down(p, w, h, gather, bm=256):
    T, K = p.shape
    D = w.shape[1]

    def body(p_ref, w_ref, h_ref, o_ref):
        o_ref[...] = h_ref[...] + dot(p_ref[...], w_ref[...], NN).astype(BF16)

    row = lambda i: (i, 0)
    o = pl.BlockSpec((bm, D), row)
    return call(
        body, (T // bm,), [pl.BlockSpec((bm, K), row), pl.BlockSpec((K, D), lambda i: (0, 0), pipeline_mode=ONE), o],
        [(o, shape((T, D), BF16))], 2 * T * K * D, T * K * 2, gather=gather,
    )(p, w, h)


def normed(h, gather=None, bm=256):
    T, D = h.shape
    b = D // 8

    def body(h_ref, o_ref, t_ref):
        wide = h_ref[...].astype(F32)
        scale = lax.rsqrt(jnp.mean(wide**2, -1, keepdims=True) + 1e-6)
        o_ref[...] = (wide * scale).astype(BF16)
        me, nxt, prv, _ = place()
        opp = 6 - me + 2 * (me % 2)
        for i, d in enumerate((opp, prv, nxt, me)):
            for j, block in ((i, d + 1 - 2 * (d % 2)), (i + 4, d)):
                t_ref[j * b:(j + 1) * b, :] = o_ref[:, pl.ds(pl.multiple_of(block * b, b), b)].T

    o = pl.BlockSpec((bm, D), lambda i: (i, 0))
    return call(
        body, (T // bm,), [o], [(o, shape((T, D), BF16)), (pl.BlockSpec((D, bm), lambda i: (0, i)), shape((D, T), BF16))],
        T * D * 8, T * D * 6, gather=gather,
    )(h)


def after(t, *before):
    return lax.optimization_barrier((t, *before))[0]


def started(s):
    oa, ob, la, lb, ra, rb, own = s
    return (sent(oa, RIGHT), sent(ob, LEFT), sent(rb, RIGHT), sent(la, LEFT), ra, lb, own)


def joined(s, *before):
    from_left, from_right, far_l, far_r, ra, lb, own, *_ = lax.optimization_barrier((*s, *before))
    to_right = (ra.astype(F32) + from_left.astype(F32)).astype(BF16)
    to_left = (lb.astype(F32) + from_right.astype(F32)).astype(BF16)
    return (to_right, to_left), (sent(to_right, RIGHT), sent(to_left, LEFT), far_l, far_r, own)


def ended(s, *before):
    near_l, near_r, far_l, far_r, own, *_ = lax.optimization_barrier((*s, *before))
    h = own.shape[0] // 2
    top = own[:h].astype(F32) + near_l.astype(F32) + far_r.astype(F32)
    low = own[h:].astype(F32) + far_l.astype(F32) + near_r.astype(F32)
    return jnp.concatenate([top, low]).astype(BF16)


PARTS = (2560, 2304, 1280)


def solution(mesh):
    def body(x, dy, wg, wu, wd):
        order = jnp.asarray(ORDER, jnp.int32)[lax.axis_index("dp")]
        theirs, mine = order[:4], order[4:]
        h0, dy = x[0], dy[0]
        n, FF = wg.shape[1], wg.shape[2]
        own = FF // 8
        offsets = [sum(PARTS[:c]) for c in range(len(PARTS))]
        first, second = lambda r: r.at[0], lambda r: r.at[1]
        cols = lambda c: lambda r: r.at[1, :, pl.ds(offsets[c], PARTS[c])]
        gu = lambda c: [(w, cols(c), (n, PARTS[c])) for w in (wg, wu)]
        a0, at0, wg0, wu0 = normed(h0, Gather(0, [(wg, first, (n, None)), (wu, first, (n, None))], [(7, 8), (7, 8)]))
        act0, u0, g0, wd0, *w1 = gateup(a0, wg0, wu0, Gather(1, [(wd, first, (own, None)), *gu(0)], [(14, 24), (20, 24), (23, 24)]))
        h1, wd1 = down(act0, wd0, h0, Gather(2, [(wd, second, (own, None))], [(7, 8)]))
        a1, at1 = normed(h1)
        act1, du, dg, *w2 = both(a1, dy, *w1, wd1, offsets[0], Gather(3, gu(1), [(3, 8), (6, 10)]), ())
        act1, du, dg, *w3 = both(a1, dy, *w2, wd1, offsets[1], Gather(4, gu(2), [(2, 5), (4, 6)]), (act1, du, dg))
        act1, du, dg = both(a1, dy, *w3, wd1, offsets[2], None, (act1, du, dg))
        wgs, wus = [w1[0], w2[0], w3[0]], [w1[1], w2[1], w3[1]]

        pd = by_blocks(theirs, act1, dy)
        xd = sent(pd, ACROSS)
        pg = by_rows(at1, after(dg, pd), 0)
        xg = sent(pg, ACROSS)
        sd = by_blocks(mine, act1, after(dy, pg), xd)
        rd = started(sd)
        pu = by_rows(at1, after(du, *sd), 0)
        xu = sent(pu, ACROSS)
        sg = by_rows(at1, after(dg, pu), 1, xg)
        rg = started(sg)
        jd, rd = joined(rd, *sg)
        su = by_rows(at1, after(du, *jd), 1, xu)
        ru = started(su)
        part = dnormed(after(dg, *su), wgs, du, wus, h1, dy, 0, 4, ())
        jg, rg = joined(rg, part)
        dwd1 = ended(rd, part)
        d1 = dnormed(after(dg, part, dwd1, *jg), wgs, du, wus, h1, dy, 4, 4, (part,))
        ju, ru = joined(ru, d1)
        d1 = after(d1, *ju)
        pd = by_blocks(theirs, act0, d1)
        xd = sent(pd, ACROSS)
        dwg1 = ended(rg, pd)

        du, dg = dproduct(after(d1, pd, dwg1), wd0, u0, g0)
        dwu1 = ended(ru, dg)
        sd = by_blocks(mine, act0, after(d1, dg, dwu1), xd)
        rd = started(sd)
        pg = by_rows(at0, after(dg, *sd), 0)
        xg = sent(pg, ACROSS)
        pu = by_rows(at0, after(du, pg), 0)
        xu = sent(pu, ACROSS)
        jd, rd = joined(rd, pu)
        sg = by_rows(at0, after(dg, *jd), 1, xg)
        rg = started(sg)
        su = by_rows(at0, after(du, *sg), 1, xu)
        ru = started(su)
        dwd0 = ended(rd, *su)
        dwd = jnp.stack([dwd0, dwd1])
        part = dnormed(after(dg, dwd, *su), [wg0], du, [wu0], h0, d1, 0, 5, ())
        jg, rg = joined(rg, part)
        ju, ru = joined(ru, part)
        d0 = dnormed(after(dg, part, *jg, *ju), [wg0], du, [wu0], h0, d1, 5, 3, (part,))
        dwg0, dwu0 = ended(rg, d0), ended(ru, d0)
        return d0[None], jnp.stack([dwg0, dwg1]), jnp.stack([dwu0, dwu1]), dwd

    data, rows = P(("rep", "dp"), None, None), P(None, "dp", None)
    out = P("rep", "dp", None)
    return jax.shard_map(body, mesh=mesh, in_specs=(data, data, rows, rows, rows), out_specs=(data, out, out, out), check_vma=False)
```

time: 1460 us -> 1070 us (0.73)
  Pallas kernels: 0 us -> 866 us
  matrix products: 659 us -> 0 us
  waiting for transfers between devices: 554 us -> 107 us
  other arithmetic: 184 us -> 48.8 us
  starting transfers between devices: 0.49 us -> 37.5 us
  local copies, waits for them, and re-layouts: 36.9 us -> 1.67 us
    pallas_call x0 -> x24, Pallas kernels: none -> 866 us  [run(): got = made(*args, *kept, *(u[0] for u in units))]
    dot_general x17 -> x0, matrix products: 659 us -> none  [the longest x6 247 us: layer(): up = jnp.dot(a, w['w_up'], preferred_element_type=jnp.float32)]
    unnamed x18 -> x0, waiting for transfers between devices: 430 us -> none
    unnamed x3 -> x0, other arithmetic: 147 us -> none
    squeeze x6 -> x0, waiting for transfers between devices: 124 us -> none  [stack(): h = layer(h, {name: w[number] for name, w in weights.items()})]
    ppermute x0 -> x42, waiting for transfers between devices: none -> 107 us  [sent(): return lax.ppermute(t, 'dp', pairs)]
    ppermute x0 -> x42, starting transfers between devices: none -> 37.5 us  [sent(): return lax.ppermute(t, 'dp', pairs)]
    unnamed x37 -> x48, local copies, waits for them, and re-layouts: 27 us -> 0.39 us
  transfers between devices with their start and end apart: 12 -> 42, of which waited for: 7 -> 10; matrix products, arithmetic and copies ran while one was open for 60% -> 3% of each run, Pallas kernels for 0% -> 35%
where the time goes in v1:
time: 1070 us; the launch traced here: 1060 us
  Pallas kernels  866 us (81%)
  waiting for transfers between devices  107 us (10%)
  other arithmetic  48.8 us (5%)
  starting transfers between devices  37.5 us (4%)
    pallas_call x24, Pallas kernels, run(): got = made(*args, *kept, *(u[0] for u in units))  866 us
    ppermute x42, waiting for transfers between devices, sent(): return lax.ppermute(t, 'dp', pairs)  107 us
    ppermute x42, starting transfers between devices, sent(): return lax.ppermute(t, 'dp', pairs)  37.5 us
  transfers between devices with their start and end apart: 42, of which 10 were waited for; matrix products, arithmetic and copies ran while one was open for 3% of the time, Pallas kernels for 35%

profile of v1, /device:TPU:0, one launch (start us, length us, event | category | flops | bytes accessed | tf_op | source)
XLA Modules:
  0.0 1061.9 jit_solution(12410813276610913930)
XLA Ops:
  0.6 112.5 %shard_map.93 = (bf16[2048,1024]{1,0:T(8,128)(2,1)}, bf16[1024,2048]{1,0:T(8,128)(2,1)}, bf16[1024,6144]{1,0:T(8,128)(2,1)}, bf16[1024,6144]{1,0:T(8,128)(2,1)}) custom-call(bf16[2048,1024]{1,0:T(8,128)(2,1)} %bitcast.31, bf16[2,128,6144]{2,1,0:T(8,128)(2,1)} %refs_8_.1, bf16[2,128,6144]{2,1,0:T(8,128)(2,1)} %refs_9_.1), custom_call_target="tpu_custom_call" | custom-call | flops 16777216 | bytes 12582912 | tf_op jit(solution)/shard_map/pallas_call | solution.py:148
  113.1 103.7 %shard_map.94 = (bf16[2048,6144]{1,0:T(8,128)(2,1)}, f32[2048,6144]{1,0:T(8,128)}, f32[2048,6144]{1,0:T(8,128)}, bf16[6144,1024]{1,0:T(8,128)(2,1)}, bf16[1024,2...) custom-call(bf16[2048,1024]{1,0:T(8,128)(2,1)} %get-tuple-element.163.refs_0_, ...), custom_call_target="tpu_custom_call" | custom-call | flops 51539607552 | bytes 125829120 | tf_op jit(solution)/shard_map/pallas_call | solution.py:148
  216.8 65.6 %shard_map.95 = (bf16[2048,1024]{1,0:T(8,128)(2,1)}, bf16[6144,1024]{1,0:T(8,128)(2,1)}) custom-call(bf16[2048,6144]{1,0:T(8,128)(2,1)} %get-tuple-element.166.refs_0_, bf16[6144,1024]{1,0:T(8,128)(2,1)} %get-tuple-element.167.refs_1_.w_ref, bf16[2048,1024]{1,0:T(8,128)(2,1)} %bitcast.32, bf16[2,768,1024]{2,1,0:T(8,128)(2,1)} %refs_3_.3), custom_call_target="tpu_custom_call" | custom-call | flops 25769803776 | bytes 25165824 | tf_op jit(solution)/shard_map/pallas_call | solution.py:148
  292.1 52.3 %shard_map.97 = (bf16[2048,6144]{1,0:T(8,128)(2,1)}, bf16[2048,6144]{1,0:T(8,128)(2,1)}, bf16[2048,6144]{1,0:T(8,128)(2,1)}, bf16[1024,2304]{1,0:T(8,128)(2,1)}, bf16[1024,2304]{1,0:T(8,128)(2,1)}) custom-call(bf16[2048,1024]{1,0:T(8,128)(2,1)} %get-tuple-element.169.refs_0_, bf16[2048,1024]{1,0:T(8,128)(2,1)} %bitcast.35, ...), custom_call_target="tpu_custom_call" | custom-call | flops 32212254720 | bytes 31457280 | tf_op jit(solution)/shard_map/pallas_call | solution.py:148
  344.5 44.1 %shard_map.98 = (bf16[2048,6144]{1,0:T(8,128)(2,1)}, bf16[2048,6144]{1,0:T(8,128)(2,1)}, bf16[2048,6144]{1,0:T(8,128)(2,1)}, bf16[1024,1280]{1,0:T(8,128)(2,1)}, bf16[1024,1280]{1,0:T(8,128)(2,1)}) custom-call(bf16[2048,1024]{1,0:T(8,128)(2,1)} %get-tuple-element.169.refs_0_, ...), custom_call_target="tpu_custom_call", output_to_operand_aliasing={{0}: (5, {}), {1}: (6, {}), {2}: (7, {})} | custom-call | flops 28991029248 | bytes 28311552 | tf_op jit(solution)/shard_map/pallas_call | solution.py:148
  388.6 24.0 %shard_map.99 = (bf16[2048,6144]{1,0:T(8,128)(2,1)}, bf16[2048,6144]{1,0:T(8,128)(2,1)}, bf16[2048,6144]{1,0:T(8,128)(2,1)}) custom-call(bf16[2048,1024]{1,0:T(8,128)(2,1)} %get-tuple-element.169.refs_0_, bf16[2048,1024]{1,0:T(8,128)(2,1)} %bitcast.37, ...), custom_call_target="tpu_custom_call", output_to_operand_aliasing={{0}: (5, {}), {1}: (6, {}), {2}: (7, {})} | custom-call | flops 16106127360 | bytes 15728640 | tf_op jit(solution)/shard_map/pallas_call | solution.py:148
  412.6 18.8 %shard_map.100 = bf16[3072,1024]{1,0:T(8,128)(2,1)} custom-call(s32[4]{0:T(128)} %get-tuple-element.334.order_ref, bf16[2048,6144]{1,0:T(8,128)(2,1)} %get-tuple-element.186.refs_0_, bf16[2048,1024]{1,0:T(8,128)(2,1)} %bitcast.38), custom_call_target="tpu_custom_call" | custom-call | flops 12884901888 | bytes 12582912 | tf_op jit(solution)/shard_map/pallas_call | solution.py:148
  431.5 18.5 %shard_map.101 = bf16[512,6144]{1,0:T(8,128)(2,1)} custom-call(bf16[1024,2048]{1,0:T(8,128)(2,1)} %get-tuple-element.184.a_ref, bf16[2048,6144]{1,0:T(8,128)(2,1)} %get-tuple-element.222.d_ref.dg_ref.refs_0_), custom_call_target="tpu_custom_call" | custom-call | flops 12884901888 | bytes 25165824 | tf_op jit(solution)/shard_map/pallas_call | solution.py:148
  450.5 21.6 %shard_map.102 = (bf16[384,1024]{1,0:T(8,128)(2,1)}, bf16[384,1024]{1,0:T(8,128)(2,1)}, bf16[384,1024]{1,0:T(8,128)(2,1)}, bf16[384,1024]{1,0:T(8,128)(2,1)}, bf...) custom-call(s32[4]{0:T(128)} %get-tuple-element.335.order_ref, ...), custom_call_target="tpu_custom_call" | custom-call | flops 12884901888 | bytes 12582912 | tf_op jit(solution)/shard_map/pallas_call | solution.py:148
  472.0 18.6 %shard_map.103 = bf16[512,6144]{1,0:T(8,128)(2,1)} custom-call(bf16[1024,2048]{1,0:T(8,128)(2,1)} %get-tuple-element.184.a_ref, bf16[2048,6144]{1,0:T(8,128)(2,1)} %get-tuple-element.209.d_ref.du_ref.refs_1_), custom_call_target="tpu_custom_call" | custom-call | flops 12884901888 | bytes 25165824 | tf_op jit(solution)/shard_map/pallas_call | solution.py:148
  494.6 19.1 %shard_map.104 = (bf16[64,6144]{1,0:T(8,128)(2,1)}, bf16[64,6144]{1,0:T(8,128)(2,1)}, bf16[64,6144]{1,0:T(8,128)(2,1)}, bf16[64,6144]{1,0:T(8,128)(2,1)}, bf16[6...) custom-call(bf16[1024,2048]{1,0:T(8,128)(2,1)} %get-tuple-element.184.a_ref, ...), custom_call_target="tpu_custom_call" | custom-call | flops 12884901888 | bytes 25165824 | tf_op jit(solution)/shard_map/pallas_call | solution.py:148
  536.1 19.1 %shard_map.105 = (bf16[64,6144]{1,0:T(8,128)(2,1)}, bf16[64,6144]{1,0:T(8,128)(2,1)}, bf16[64,6144]{1,0:T(8,128)(2,1)}, bf16[64,6144]{1,0:T(8,128)(2,1)}, bf16[6...) custom-call(bf16[1024,2048]{1,0:T(8,128)(2,1)} %get-tuple-element.184.a_ref, ...), custom_call_target="tpu_custom_call" | custom-call | flops 12884901888 | bytes 25165824 | tf_op jit(solution)/shard_map/pallas_call | solution.py:148
  555.1 39.9 %shard_map.106.refs_10_ = bf16[2048,1024]{1,0:T(8,128)(2,1)} custom-call(bf16[2048,6144]{1,0:T(8,128)(2,1)} %get-tuple-element.222.d_ref.dg_ref.refs_0_, bf16[2048,6144]{1,0:T(8,128)(2,1)} %get-tuple-element.209.d_ref.du_ref.refs_1_, bf16[1024,2560]{1,0:T(8,128)(2,1)} %get-tuple-element.170.refs_2_.refs_0_, ...), custom_call_target="tpu_custom_call" | custom-call | flops 25769803776 | bytes 25165824 | tf_op jit(solution)/shard_map/pallas_call | solution.py:148
  615.8 39.8 %shard_map.107.refs_1_.d_ref.refs_3_.refs_5_ = bf16[2048,1024]{1,0:T(8,128)(2,1)} custom-call(bf16[2048,6144]{1,0:T(8,128)(2,1)} %get-tuple-element.222.d_ref.dg_ref.refs_0_, bf16[2048,6144]{1,0:T(8,128)(2,1)} %get-tuple-element.209.d_ref.du_ref.refs_1_, bf16[1024,2560]{1,0:T(8,128)(2,1)} %get-tuple-element.170.refs_2_.refs_0_, ...), custom_call_target="tpu_custom_call", output_to_operand_aliasing={{}: (10, {})} | custom-call | flops 25769803776 | bytes 25165824 | tf_op jit(solution)/shard_map/pallas_call | solution.py:148
  660.6 19.2 %shard_map.108 = bf16[3072,1024]{1,0:T(8,128)(2,1)} custom-call(s32[4]{0:T(128)} %get-tuple-element.334.order_ref, bf16[2048,6144]{1,0:T(8,128)(2,1)} %get-tuple-element.166.refs_0_, bf16[2048,1024]{1,0:T(8,128)(2,1)} %shard_map.107.refs_1_.d_ref.refs_3_.refs_5_), custom_call_target="tpu_custom_call" | custom-call | flops 12884901888 | bytes 12582912 | tf_op jit(solution)/shard_map/pallas_call | solution.py:148
  679.8 61.7 %shard_map.109 = (bf16[2048,6144]{1,0:T(8,128)(2,1)}, bf16[2048,6144]{1,0:T(8,128)(2,1)}) custom-call(bf16[2048,1024]{1,0:T(8,128)(2,1)} %shard_map.107.refs_1_.d_ref.refs_3_.refs_5_, bf16[6144,1024]{1,0:T(8,128)(2,1)} %get-tuple-element.167.refs_1_.w_ref, f32[2048,6144]{1,0:T(8,128)} %get-tuple-element.229.u_ref, f32[2048,6144]{1,0:T(8,128)} %get-tuple-element.230.g_ref), custom_call_target="tpu_custom_call" | custom-call | flops 25769803776 | bytes 150994944 | tf_op jit(solution)/shard_map/pallas_call | solution.py:148
  741.6 21.4 %shard_map.110 = (bf16[384,1024]{1,0:T(8,128)(2,1)}, bf16[384,1024]{1,0:T(8,128)(2,1)}, bf16[384,1024]{1,0:T(8,128)(2,1)}, bf16[384,1024]{1,0:T(8,128)(2,1)}, bf...) custom-call(s32[4]{0:T(128)} %get-tuple-element.335.order_ref, ...), custom_call_target="tpu_custom_call" | custom-call | flops 12884901888 | bytes 12582912 | tf_op jit(solution)/shard_map/pallas_call | solution.py:148
  762.9 18.5 %shard_map.111 = bf16[512,6144]{1,0:T(8,128)(2,1)} custom-call(bf16[1024,2048]{1,0:T(8,128)(2,1)} %get-tuple-element.240.a_ref, bf16[2048,6144]{1,0:T(8,128)(2,1)} %get-tuple-element.289.d_ref.dg_ref.refs_0_), custom_call_target="tpu_custom_call" | custom-call | flops 12884901888 | bytes 25165824 | tf_op jit(solution)/shard_map/pallas_call | solution.py:148
  781.9 18.7 %shard_map.112 = bf16[512,6144]{1,0:T(8,128)(2,1)} custom-call(bf16[1024,2048]{1,0:T(8,128)(2,1)} %get-tuple-element.240.a_ref, bf16[2048,6144]{1,0:T(8,128)(2,1)} %get-tuple-element.259.d_ref.du_ref.refs_1_), custom_call_target="tpu_custom_call" | custom-call | flops 12884901888 | bytes 25165824 | tf_op jit(solution)/shard_map/pallas_call | solution.py:148
  803.8 17.4 %collective-permute-done.37 = bf16[64,6144]{1,0:T(8,128)(2,1)S(1)} collective-permute-done((bf16[64,6144]{1,0:T(8,128)(2,1)S(1)}, bf16[64,6144]{1,0:T(8,128)(2,1)S(1)}, u32[]{:S(2)}, u32[]{:S(2)}) %collective-permute-start.37) | collective-permute-done | bytes 786464 | tf_op jit(solution)/shard_map/ppermute | solution.py:221
  878.9 19.1 %shard_map.113 = (bf16[64,6144]{1,0:T(8,128)(2,1)}, bf16[64,6144]{1,0:T(8,128)(2,1)}, bf16[64,6144]{1,0:T(8,128)(2,1)}, bf16[64,6144]{1,0:T(8,128)(2,1)}, bf16[6...) custom-call(bf16[1024,2048]{1,0:T(8,128)(2,1)} %get-tuple-element.240.a_ref, ...), custom_call_target="tpu_custom_call" | custom-call | flops 12884901888 | bytes 25165824 | tf_op jit(solution)/shard_map/pallas_call | solution.py:148
  899.0 19.1 %shard_map.114 = (bf16[64,6144]{1,0:T(8,128)(2,1)}, bf16[64,6144]{1,0:T(8,128)(2,1)}, bf16[64,6144]{1,0:T(8,128)(2,1)}, bf16[64,6144]{1,0:T(8,128)(2,1)}, bf16[6...) custom-call(bf16[1024,2048]{1,0:T(8,128)(2,1)} %get-tuple-element.240.a_ref, ...), custom_call_target="tpu_custom_call" | custom-call | flops 12884901888 | bytes 25165824 | tf_op jit(solution)/shard_map/pallas_call | solution.py:148
  956.7 48.0 %shard_map.115.refs_6_ = bf16[2048,1024]{1,0:T(8,128)(2,1)} custom-call(bf16[2048,6144]{1,0:T(8,128)(2,1)} %get-tuple-element.289.d_ref.dg_ref.refs_0_, bf16[2048,6144]{1,0:T(8,128)(2,1)} %get-tuple-element.259.d_ref.du_ref.refs_1_, bf16[1024,6144]{1,0:T(8,128)(2,1)} %get-tuple-element.164.refs_1_.refs_0_.refs_2_, ...), custom_call_target="tpu_custom_call" | custom-call | flops 32212254720 | bytes 31457280 | tf_op jit(solution)/shard_map/pallas_call | solution.py:148
  1017.9 34.0 %shard_map.116 = bf16[2048,1024]{1,0:T(8,128)(2,1)} custom-call(bf16[2048,6144]{1,0:T(8,128)(2,1)} %get-tuple-element.289.d_ref.dg_ref.refs_0_, bf16[2048,6144]{1,0:T(8,128)(2,1)} %get-tuple-element.259.d_ref.du_ref.refs_1_, bf16[1024,6144]{1,0:T(8,128)(2,1)} %get-tuple-element.164.refs_1_.refs_0_.refs_2_, ...), custom_call_target="tpu_custom_call", output_to_operand_aliasing={{}: (6, {})} | custom-call | flops 19327352832 | bytes 18874368 | tf_op jit(solution)/shard_map/pallas_call | solution.py:148
  (154 shorter events, 186.1 us)
Async XLA Ops:
  450.0 43.7 %collective-permute-start.5 = (bf16[512,6144]{1,0:T(8,128)(2,1)}, bf16[512,6144]{1,0:T(8,128)(2,1)}, u32[]{:S(2)}, u32[]{:S(2)}) collective-permute-start(bf16[512,6144]{1,0:T(8,128)(2,1)} %shard_map.101), channel_id=1, source_target_pairs={{0,1},{1,0},{2,3},{3,2},{4,5},{5,4},{6,7},{7,6}} | collective-permute-start | bytes 18874376 | tf_op jit(solution)/shard_map/ppermute | solution.py:221
  490.6 44.4 %collective-permute-start.6 = (bf16[512,6144]{1,0:T(8,128)(2,1)}, bf16[512,6144]{1,0:T(8,128)(2,1)}, u32[]{:S(2)}, u32[]{:S(2)}) collective-permute-start(bf16[512,6144]{1,0:T(8,128)(2,1)} %shard_map.103), channel_id=1, source_target_pairs={{0,1},{1,0},{2,3},{3,2},{4,5},{5,4},{6,7},{7,6}} | collective-permute-start | bytes 18874376 | tf_op jit(solution)/shard_map/ppermute | solution.py:221
  513.7 81.3 %collective-permute-start.10 = (bf16[64,6144]{1,0:T(8,128)(2,1)}, bf16[64,6144]{1,0:T(8,128)(2,1)}, u32[]{:S(2)}, u32[]{:S(2)}) collective-permute-start(bf16[64,6144]{1,0:T(8,128)(2,1)} %get-tuple-element.200), channel_id=1, source_target_pairs={{0,4},{1,5},{2,0},{3,1},{4,6},{5,7},{6,2},{7,3}} | collective-permute-start | bytes 2359304 | tf_op jit(solution)/shard_map/ppermute | solution.py:221
  514.8 81.2 %collective-permute-start.7 = (bf16[64,6144]{1,0:T(8,128)(2,1)}, bf16[64,6144]{1,0:T(8,128)(2,1)}, u32[]{:S(2)}, u32[]{:S(2)}) collective-permute-start(bf16[64,6144]{1,0:T(8,128)(2,1)} %get-tuple-element.198), channel_id=1, source_target_pairs={{0,2},{1,3},{2,6},{3,7},{4,0},{5,1},{6,4},{7,5}} | collective-permute-start | bytes 2359304 | tf_op jit(solution)/shard_map/ppermute | solution.py:221
  528.1 69.0 %collective-permute-start.8 = (bf16[64,6144]{1,0:T(8,128)(2,1)}, bf16[64,6144]{1,0:T(8,128)(2,1)}, u32[]{:S(2)}, u32[]{:S(2)}) collective-permute-start(bf16[64,6144]{1,0:T(8,128)(2,1)} %get-tuple-element.199), channel_id=1, source_target_pairs={{0,4},{1,5},{2,0},{3,1},{4,6},{5,7},{6,2},{7,3}} | collective-permute-start | bytes 2359304 | tf_op jit(solution)/shard_map/ppermute | solution.py:221
  529.1 68.9 %collective-permute-start.9 = (bf16[64,6144]{1,0:T(8,128)(2,1)}, bf16[64,6144]{1,0:T(8,128)(2,1)}, u32[]{:S(2)}, u32[]{:S(2)}) collective-permute-start(bf16[64,6144]{1,0:T(8,128)(2,1)} %get-tuple-element.203), channel_id=1, source_target_pairs={{0,2},{1,3},{2,6},{3,7},{4,0},{5,1},{6,4},{7,5}} | collective-permute-start | bytes 2359304 | tf_op jit(solution)/shard_map/ppermute | solution.py:221
  535.0 68.8 %collective-permute-start.25 = (bf16[384,1024]{1,0:T(8,128)(2,1)}, bf16[384,1024]{1,0:T(8,128)(2,1)S(1)}, u32[]{:S(2)}, u32[]{:S(2)}) collective-permute-start(bf16[384,1024]{1,0:T(8,128)(2,1)} %add_convert_fusion.22), channel_id=1, source_target_pairs={{0,4},{1,5},{2,0},{3,1},{4,6},{5,7},{6,2},{7,3}} | collective-permute-start | bytes 2359304 | tf_op jit(solution)/shard_map/ppermute | solution.py:221
  596.0 59.5 %collective-permute-start.11 = (bf16[64,6144]{1,0:T(8,128)(2,1)}, bf16[64,6144]{1,0:T(8,128)(2,1)}, u32[]{:S(2)}, u32[]{:S(2)}) collective-permute-start(bf16[64,6144]{1,0:T(8,128)(2,1)} %get-tuple-element.210), channel_id=1, source_target_pairs={{0,2},{1,3},{2,6},{3,7},{4,0},{5,1},{6,4},{7,5}} | collective-permute-start | bytes 2359304 | tf_op jit(solution)/shard_map/ppermute | solution.py:221
  597.1 58.5 %collective-permute-start.12 = (bf16[64,6144]{1,0:T(8,128)(2,1)}, bf16[64,6144]{1,0:T(8,128)(2,1)}, u32[]{:S(2)}, u32[]{:S(2)}) collective-permute-start(bf16[64,6144]{1,0:T(8,128)(2,1)} %get-tuple-element.211), channel_id=1, source_target_pairs={{0,4},{1,5},{2,0},{3,1},{4,6},{5,7},{6,2},{7,3}} | collective-permute-start | bytes 2359304 | tf_op jit(solution)/shard_map/ppermute | solution.py:221
  598.1 57.5 %collective-permute-start.13 = (bf16[64,6144]{1,0:T(8,128)(2,1)}, bf16[64,6144]{1,0:T(8,128)(2,1)S(1)}, u32[]{:S(2)}, u32[]{:S(2)}) collective-permute-start(bf16[64,6144]{1,0:T(8,128)(2,1)} %get-tuple-element.215), channel_id=1, source_target_pairs={{0,2},{1,3},{2,6},{3,7},{4,0},{5,1},{6,4},{7,5}} | collective-permute-start | bytes 2359304 | tf_op jit(solution)/shard_map/ppermute | solution.py:221
  603.7 51.9 %collective-permute-start.14 = (bf16[64,6144]{1,0:T(8,128)(2,1)}, bf16[64,6144]{1,0:T(8,128)(2,1)}, u32[]{:S(2)}, u32[]{:S(2)}) collective-permute-start(bf16[64,6144]{1,0:T(8,128)(2,1)} %get-tuple-element.212), channel_id=1, source_target_pairs={{0,4},{1,5},{2,0},{3,1},{4,6},{5,7},{6,2},{7,3}} | collective-permute-start | bytes 2359304 | tf_op jit(solution)/shard_map/ppermute | solution.py:221
  679.8 61.7 %collective-permute-start.15 = (bf16[3072,1024]{1,0:T(8,128)(2,1)}, bf16[3072,1024]{1,0:T(8,128)(2,1)}, u32[]{:S(2)}, u32[]{:S(2)}) collective-permute-start(bf16[3072,1024]{1,0:T(8,128)(2,1)} %shard_map.108), channel_id=1, source_target_pairs={{0,1},{1,0},{2,3},{3,2},{4,5},{5,4},{6,7},{7,6}} | collective-permute-start | bytes 18874376 | tf_op jit(solution)/shard_map/ppermute | solution.py:221
  781.4 97.5 %collective-permute-start.22 = (bf16[512,6144]{1,0:T(8,128)(2,1)}, bf16[512,6144]{1,0:T(8,128)(2,1)}, u32[]{:S(2)}, u32[]{:S(2)}) collective-permute-start(bf16[512,6144]{1,0:T(8,128)(2,1)} %shard_map.111), channel_id=1, source_target_pairs={{0,1},{1,0},{2,3},{3,2},{4,5},{5,4},{6,7},{7,6}} | collective-permute-start | bytes 18874376 | tf_op jit(solution)/shard_map/ppermute | solution.py:221
  800.7 98.3 %collective-permute-start.23 = (bf16[512,6144]{1,0:T(8,128)(2,1)}, bf16[512,6144]{1,0:T(8,128)(2,1)}, u32[]{:S(2)}, u32[]{:S(2)}) collective-permute-start(bf16[512,6144]{1,0:T(8,128)(2,1)} %shard_map.112), channel_id=1, source_target_pairs={{0,1},{1,0},{2,3},{3,2},{4,5},{5,4},{6,7},{7,6}} | collective-permute-start | bytes 18874376 | tf_op jit(solution)/shard_map/ppermute | solution.py:221
  875.7 44.4 %collective-permute-start.21 = (bf16[384,1024]{1,0:T(8,128)(2,1)}, bf16[384,1024]{1,0:T(8,128)(2,1)}, u32[]{:S(2)}, u32[]{:S(2)}) collective-permute-start(bf16[384,1024]{1,0:T(8,128)(2,1)} %add_convert_fusion.16), channel_id=1, source_target_pairs={{0,4},{1,5},{2,0},{3,1},{4,6},{5,7},{6,2},{7,3}} | collective-permute-start | bytes 2359304 | tf_op jit(solution)/shard_map/ppermute | solution.py:221
  877.9 43.3 %collective-permute-start.20 = (bf16[384,1024]{1,0:T(8,128)(2,1)}, bf16[384,1024]{1,0:T(8,128)(2,1)}, u32[]{:S(2)}, u32[]{:S(2)}) collective-permute-start(bf16[384,1024]{1,0:T(8,128)(2,1)} %add_convert_fusion.17), channel_id=1, source_target_pairs={{0,2},{1,3},{2,6},{3,7},{4,0},{5,1},{6,4},{7,5}} | collective-permute-start | bytes 2359304 | tf_op jit(solution)/shard_map/ppermute | solution.py:221
  898.0 106.7 %collective-permute-start.26 = (bf16[64,6144]{1,0:T(8,128)(2,1)}, bf16[64,6144]{1,0:T(8,128)(2,1)}, u32[]{:S(2)}, u32[]{:S(2)}) collective-permute-start(bf16[64,6144]{1,0:T(8,128)(2,1)} %get-tuple-element.252), channel_id=1, source_target_pairs={{0,2},{1,3},{2,6},{3,7},{4,0},{5,1},{6,4},{7,5}} | collective-permute-start | bytes 2359304 | tf_op jit(solution)/shard_map/ppermute | solution.py:221
  921.2 83.5 %collective-permute-start.33 = (bf16[64,6144]{1,0:T(8,128)(2,1)}, bf16[64,6144]{1,0:T(8,128)(2,1)}, u32[]{:S(2)}, u32[]{:S(2)}) collective-permute-start(bf16[64,6144]{1,0:T(8,128)(2,1)} %get-tuple-element.262), channel_id=1, source_target_pairs={{0,4},{1,5},{2,0},{3,1},{4,6},{5,7},{6,2},{7,3}} | collective-permute-start | bytes 2359304 | tf_op jit(solution)/shard_map/ppermute | solution.py:221
  938.8 65.9 %collective-permute-start.27 = (bf16[64,6144]{1,0:T(8,128)(2,1)}, bf16[64,6144]{1,0:T(8,128)(2,1)}, u32[]{:S(2)}, u32[]{:S(2)}) collective-permute-start(bf16[64,6144]{1,0:T(8,128)(2,1)} %get-tuple-element.253), channel_id=1, source_target_pairs={{0,4},{1,5},{2,0},{3,1},{4,6},{5,7},{6,2},{7,3}} | collective-permute-start | bytes 2359304 | tf_op jit(solution)/shard_map/ppermute | solution.py:221
  939.9 64.9 %collective-permute-start.28 = (bf16[64,6144]{1,0:T(8,128)(2,1)}, bf16[64,6144]{1,0:T(8,128)(2,1)}, u32[]{:S(2)}, u32[]{:S(2)}) collective-permute-start(bf16[64,6144]{1,0:T(8,128)(2,1)} %get-tuple-element.257), channel_id=1, source_target_pairs={{0,2},{1,3},{2,6},{3,7},{4,0},{5,1},{6,4},{7,5}} | collective-permute-start | bytes 2359304 | tf_op jit(solution)/shard_map/ppermute | solution.py:221
  955.6 49.1 %collective-permute-start.29 = (bf16[64,6144]{1,0:T(8,128)(2,1)}, bf16[64,6144]{1,0:T(8,128)(2,1)}, u32[]{:S(2)}, u32[]{:S(2)}) collective-permute-start(bf16[64,6144]{1,0:T(8,128)(2,1)} %get-tuple-element.254), channel_id=1, source_target_pairs={{0,4},{1,5},{2,0},{3,1},{4,6},{5,7},{6,2},{7,3}} | collective-permute-start | bytes 2359304 | tf_op jit(solution)/shard_map/ppermute | solution.py:221
  1007.2 44.7 %collective-permute-start.39 = (bf16[64,6144]{1,0:T(8,128)(2,1)}, bf16[64,6144]{1,0:T(8,128)(2,1)}, u32[]{:S(2)}, u32[]{:S(2)}) collective-permute-start(bf16[64,6144]{1,0:T(8,128)(2,1)} %add_convert_fusion.8), channel_id=1, source_target_pairs={{0,4},{1,5},{2,0},{3,1},{4,6},{5,7},{6,2},{7,3}} | collective-permute-start | bytes 2359304 | tf_op jit(solution)/shard_map/ppermute | solution.py:221
  1010.4 41.5 %collective-permute-start.38 = (bf16[64,6144]{1,0:T(8,128)(2,1)}, bf16[64,6144]{1,0:T(8,128)(2,1)}, u32[]{:S(2)}, u32[]{:S(2)}) collective-permute-start(bf16[64,6144]{1,0:T(8,128)(2,1)} %add_convert_fusion.9), channel_id=1, source_target_pairs={{0,2},{1,3},{2,6},{3,7},{4,0},{5,1},{6,4},{7,5}} | collective-permute-start | bytes 2359304 | tf_op jit(solution)/shard_map/ppermute | solution.py:221
  1013.7 38.3 %collective-permute-start.35 = (bf16[64,6144]{1,0:T(8,128)(2,1)}, bf16[64,6144]{1,0:T(8,128)(2,1)}, u32[]{:S(2)}, u32[]{:S(2)}) collective-permute-start(bf16[64,6144]{1,0:T(8,128)(2,1)} %add_convert_fusion.10), channel_id=1, source_target_pairs={{0,4},{1,5},{2,0},{3,1},{4,6},{5,7},{6,2},{7,3}} | collective-permute-start | bytes 2359304 | tf_op jit(solution)/shard_map/ppermute | solution.py:221
  (42 other events, 955.9 us)

commit v2 on v1

--- a/solution.py
+++ b/solution.py
@@ -66,18 +66,19 @@
         self.number, self.units, self.ticks = number, units, ticks
 
 
-def call(body, grid, ins, outs, flops, nbytes, prefetch=0, gather=None, kept=(), vmem=62 * 2**20):
-    n_in, n_out, n_kept = prefetch + len(ins), len(outs), len(kept)
+def call(body, grid, ins, outs, flops, nbytes, prefetch=0, gather=None, kept=(), scratch=(), sums=(), vmem=62 * 2**20):
+    n_in, n_out, n_kept, n_main = prefetch + len(ins), len(outs), len(kept), len(outs)
+    added = [t for terms in sums for t in terms]
     hbm = pl.BlockSpec(memory_space=pl.ANY)
     units = gather.units if gather else []
-    specs, shapes, scratch, whole = list(ins) + [hbm] * n_kept, [o for _, o in outs], [], body
+    specs, shapes, scratch, whole = list(ins) + [hbm] * n_kept, [o for _, o in outs], list(scratch), body
     if gather:
         steps = grid[0]
 
         def whole(*refs):
             owns = [part(r) for r, (_, part, _) in zip(refs[n_in + n_kept:], units)]
             results = refs[n_in + n_kept + len(units):]
-            wholes, send, recv = results[n_out:n_out + len(units)], results[-2], results[-1]
+            wholes, (*mine, send, recv) = results[n_out:n_out + len(units)], results[n_out + len(units):]
             copies = [gather_copies(o, w, send.at[u], recv.at[u]) for u, (o, w) in enumerate(zip(owns, wholes))]
             step = pl.program_id(0)
 
@@ -114,7 +115,7 @@
                 pl.when(step == two)(functools.partial(second, c))
                 if three < steps:
                     pl.when(step == three)(functools.partial(third, c))
-            body(*refs[:n_in], *results[:n_out])
+            body(*refs[:n_in], *results[:n_out], *mine)
 
             @pl.when(step == steps - 1)
             def _():
@@ -126,13 +127,33 @@
         specs += [hbm] * len(units)
         outs = list(outs) + [(hbm, shape((8 * n, w.shape[-1] if cols is None else cols), BF16)) for w, _, (n, cols) in units]
         shapes = [o for _, o in outs]
-        scratch = [pltpu.SemaphoreType.DMA((len(units), 9)), pltpu.SemaphoreType.DMA((len(units), 8))]
+        scratch += [pltpu.SemaphoreType.DMA((len(units), 9)), pltpu.SemaphoreType.DMA((len(units), 8))]
         extra = dict(collective_id=gather.number, has_side_effects=True)
     else:
         extra = {}
-        if kept:
-            def whole(*refs):
-                body(*refs[:n_in], *refs[n_in + n_kept:])
+        steps = grid[0]
+
+        def piece(t):
+            r, c = t.shape
+            if c % (128 * steps) == 0:
+                return pl.BlockSpec((r, c // steps), lambda j, *_: (0, j))
+            return pl.BlockSpec((r // steps, c), lambda j, *_: (j, 0))
+
+        specs += [piece(t) for t in added]
+        outs = list(outs) + [(piece(terms[0]), shape(terms[0].shape, BF16)) for terms in sums]
+        shapes = [o for _, o in outs]
+
+        def whole(*refs):
+            terms = refs[n_in + n_kept:]
+            results = terms[len(added):]
+            at = 0
+            for o_ref, group in zip(results[n_main:], sums):
+                total = terms[at][...].astype(F32)
+                for t in terms[at + 1:at + len(group)]:
+                    total = total + t[...].astype(F32)
+                o_ref[...] = total.astype(BF16)
+                at += len(group)
+            body(*refs[:n_in], *results[:n_main], *results[n_main + len(sums):])
     made = pl.pallas_call(
         whole,
         grid_spec=pltpu.PrefetchScalarGridSpec(
@@ -145,17 +166,17 @@
     )
 
     def run(*args):
-        got = made(*args, *kept, *(u[0] for u in units))
+        got = made(*args, *kept, *added, *(u[0] for u in units))
         return got[0] if len(outs) == 1 else got
 
     return run
 
 
 def pieces(rows, cols):
-    return [(rows // 8, cols)] * 6 + [(rows // 4, cols)]
-
-
-def by_rows(at, d, half, got=None, bn=1024):
+    return [(rows // 8, cols)] * 8
+
+
+def by_rows(at, d, half, got=None, bn=1024, sums=()):
     T, N = d.shape
     rows = at.shape[0] // 2
     h = rows // 8
@@ -165,9 +186,8 @@
 
     def mine(a_ref, d_ref, got_ref, *outs):
         t = (dot(a_ref[...], d_ref[...], NN) + got_ref[...].astype(F32)).astype(BF16)
-        for i in range(6):
+        for i in range(8):
             outs[i][...] = t[i * h:(i + 1) * h, :]
-        outs[6][...] = t[6 * h:, :]
 
     col = lambda j: (0, j)
     ins = [pl.BlockSpec((rows, T), lambda j: (half, 0), pipeline_mode=ONE), pl.BlockSpec((T, bn), col)]
@@ -177,10 +197,10 @@
         args.append(got)
         results = pieces(rows, N)
     outs = [(pl.BlockSpec((r, bn), col), shape((r, N), BF16)) for r, _ in results]
-    return call(theirs if got is None else mine, (N // bn,), ins, outs, 2 * rows * T * N, T * N * 2)(*args)
-
-
-def by_blocks(order, p, d, got=None, parts=1):
+    return call(theirs if got is None else mine, (N // bn,), ins, outs, 2 * rows * T * N, T * N * 2, sums=sums)(*args)
+
+
+def by_blocks(order, p, d, got=None, parts=1, sums=()):
     T, D = d.shape
     n, bm = order.shape[0], p.shape[1] // 8
     width, h = bm // parts, bm // 2
@@ -195,15 +215,11 @@
             r = slice(c * width, (c + 1) * width)
             t = dot(refs[c][...], refs[parts][...], TN)
             refs[parts + 1][r, :] = (t + refs[parts + 1][r, :].astype(F32)).astype(BF16)
-        for i in range(3):
+        for i in range(4):
             @pl.when(step == i)
             def _():
                 outs[2 * i][...] = refs[parts + 1][:h, :]
                 outs[2 * i + 1][...] = refs[parts + 1][h:, :]
-
-        @pl.when(step == 3)
-        def _():
-            outs[6][...] = refs[parts + 1][...]
 
     ins = [pl.BlockSpec((T, width), functools.partial(lambda c, i, o: (0, c * 8 + o[i]), c)) for c in range(parts)]
     ins.append(pl.BlockSpec((T, D), lambda i, o: (0, 0), pipeline_mode=ONE))
@@ -214,7 +230,9 @@
         ins.append(block)
         args.append(got)
         outs = [(pl.BlockSpec(s, lambda i, o: (0, 0)), shape(s, BF16)) for s in pieces(n * bm, D)]
-    return call(theirs if got is None else mine, (n,), ins, outs, 2 * n * bm * T * D, T * n * bm * 2, prefetch=1)(*args)
+    return call(
+        theirs if got is None else mine, (n,), ins, outs, 2 * n * bm * T * D, T * n * bm * 2, prefetch=1, sums=sums
+    )(*args)
 
 
 def sent(t, pairs):
@@ -244,22 +262,42 @@
     )(a, wg, wu)
 
 
+def loaded(sources, targets, sems):
+    copies = [pltpu.make_async_copy(s, t, sems.at[i]) for i, (s, t) in enumerate(zip(sources, targets))]
+    for c in copies:
+        c.start()
+    return lambda i: copies[i].wait()
+
+
 def dproduct(dy, wd, by_u, by_g, bm=256, bn=1024):
     T, D = dy.shape
     N = wd.shape[0]
-
-    def body(d_ref, w_ref, u_ref, g_ref, du_ref, dg_ref):
-        for i in range(N // bn):
-            r = slice(i * bn, (i + 1) * bn)
-            dp = dot(d_ref[...], w_ref[r, :], NT).astype(BF16).astype(F32)
-            du_ref[:, r] = (dp * u_ref[:, r]).astype(BF16)
-            dg_ref[:, r] = (dp * g_ref[:, r] * 2.0).astype(BF16)
+    n = N // bn
+
+    def body(d_ref, w_hbm, u_ref, g_ref, du_ref, dg_ref, w_ref, sems):
+        def all_of(wait):
+            for i in range(n):
+                wait(i)
+                r = slice(i * bn, (i + 1) * bn)
+                dp = dot(d_ref[...], w_ref[r, :], NT).astype(BF16).astype(F32)
+                du_ref[:, r] = (dp * u_ref[:, r]).astype(BF16)
+                dg_ref[:, r] = (dp * g_ref[:, r] * 2.0).astype(BF16)
+
+        @pl.when(pl.program_id(0) == 0)
+        def _():
+            cuts = [pl.ds(i * bn, bn) for i in range(n)]
+            all_of(loaded([w_hbm.at[c] for c in cuts], [w_ref.at[c] for c in cuts], sems))
+
+        @pl.when(pl.program_id(0) != 0)
+        def _():
+            all_of(lambda i: None)
 
     row = lambda j: (j, 0)
     o = pl.BlockSpec((bm, N), row)
     return call(
-        body, (T // bm,), [pl.BlockSpec((bm, D), row), pl.BlockSpec((N, D), lambda j: (0, 0), pipeline_mode=ONE), o, o],
+        body, (T // bm,), [pl.BlockSpec((bm, D), row), pl.BlockSpec(memory_space=pl.ANY), o, o],
         [(o, shape((T, N), BF16)), (o, shape((T, N), BF16))], 2 * T * D * N, T * N * 12,
+        scratch=[pltpu.VMEM((N, D), BF16), pltpu.SemaphoreType.DMA((n,))],
     )(dy, wd, by_u, by_g)
 
 
@@ -288,46 +326,80 @@
     )(a, dy, wg, wu, wd)
 
 
-def dnormed(dg, wgs, du, wus, h, g, start, steps, kept, bm=256):
+def dnormed(dg, wgs, du, wus, h, g, start, steps, kept, sums=(), bm=256):
     n = len(wgs)
     T, K = dg.shape
     D = wgs[0].shape[0]
-
-    def product(d_ref, refs):
-        total, at = None, 0
-        for r in refs:
-            t = dot(d_ref[:, at:at + r.shape[1]], r[...], NT)
-            total, at = t if total is None else total + t, at + r.shape[1]
-        return total.astype(BF16)
+    cuts, at = [], 0
+    for p, w in enumerate(wgs):
+        each = next(c for c in (1280, 1152, 1024) if w.shape[1] % c == 0)
+        for i in range(w.shape[1] // each):
+            cuts.append((p, i * each, at + i * each, each))
+        at += w.shape[1]
 
     def body(dg_ref, du_ref, *refs):
-        h_ref, g_ref, o_ref = refs[2 * n:]
-        da = (product(dg_ref, refs[:n]) + product(du_ref, refs[n:2 * n])).astype(F32)
-        wide = h_ref[...].astype(F32)
+        h_ref, g_ref, o_ref, wg_ref, wu_ref, da_ref, sems = refs[2 * n:]
+
+        @pl.when(pl.program_id(0) == 0)
+        def _():
+            sources = [refs[m * n + p].at[:, pl.ds(c, w)] for m in range(2) for p, c, _, w in cuts]
+            targets = [r.at[:, pl.ds(c, w)] for r in (wg_ref, wu_ref) for _, _, c, w in cuts]
+            wait = loaded(sources, targets, sems)
+            sums = []
+            for m, (d_ref, w_ref) in enumerate(((dg_ref, wg_ref), (du_ref, wu_ref))):
+                total = None
+                for i, (_, _, c, w) in enumerate(cuts):
+                    wait(m * len(cuts) + i)
+                    t = dot(d_ref[:, c:c + w], w_ref[:, c:c + w], NT)
+                    total = t if total is None else total + t
+                sums.append(total.astype(BF16))
+            da_ref[...] = sums[0] + sums[1]
+
+        @pl.when(pl.program_id(0) != 0)
+        def _():
+            da_ref[...] = dot(dg_ref[...], wg_ref[...], NT).astype(BF16) + dot(du_ref[...], wu_ref[...], NT).astype(BF16)
+
+        da, wide = da_ref[...].astype(F32), h_ref[...].astype(F32)
         scale = lax.rsqrt(jnp.mean(wide**2, -1, keepdims=True) + 1e-6)
         inner = jnp.mean(da * wide, -1, keepdims=True)
         o_ref[...] = g_ref[...] + (da * scale - wide * (scale * scale * scale * inner)).astype(BF16)
 
     row = lambda i: (start + i, 0)
-    full = [pl.BlockSpec(w.shape, lambda i: (0, 0), pipeline_mode=ONE) for w in (*wgs, *wus)]
     d, o = pl.BlockSpec((bm, K), row), pl.BlockSpec((bm, D), row)
     return call(
-        body, (steps,), [d, d, *full, o, o], [(o, shape((T, D), BF16))], 4 * steps * bm * K * D, steps * bm * K * 4, kept=kept,
+        body, (steps,), [d, d, *[pl.BlockSpec(memory_space=pl.ANY)] * (2 * n), o, o], [(o, shape((T, D), BF16))],
+        4 * steps * bm * K * D, steps * bm * K * 4, kept=kept, sums=sums,
+        scratch=[pltpu.VMEM((D, K), BF16)] * 2 + [pltpu.VMEM((bm, D), BF16), pltpu.SemaphoreType.DMA((2 * len(cuts),))],
     )(dg, du, *wgs, *wus, h, g)
 
 
-def down(p, w, h, gather, bm=256):
+def down(p, w, h, gather, bm=256, bk=1024):
     T, K = p.shape
     D = w.shape[1]
-
-    def body(p_ref, w_ref, h_ref, o_ref):
-        o_ref[...] = h_ref[...] + dot(p_ref[...], w_ref[...], NN).astype(BF16)
+    n = K // bk
+
+    def body(p_ref, w_hbm, h_ref, o_ref, w_ref, sems):
+        @pl.when(pl.program_id(0) == 0)
+        def _():
+            cuts = [pl.ds(i * bk, bk) for i in range(n)]
+            wait = loaded([w_hbm.at[c] for c in cuts], [w_ref.at[c] for c in cuts], sems)
+            total = None
+            for i in range(n):
+                wait(i)
+                t = dot(p_ref[:, i * bk:(i + 1) * bk], w_ref[i * bk:(i + 1) * bk, :], NN)
+                total = t if total is None else total + t
+            o_ref[...] = h_ref[...] + total.astype(BF16)
+
+        @pl.when(pl.program_id(0) != 0)
+        def _():
+            o_ref[...] = h_ref[...] + dot(p_ref[...], w_ref[...], NN).astype(BF16)
 
     row = lambda i: (i, 0)
     o = pl.BlockSpec((bm, D), row)
     return call(
-        body, (T // bm,), [pl.BlockSpec((bm, K), row), pl.BlockSpec((K, D), lambda i: (0, 0), pipeline_mode=ONE), o],
+        body, (T // bm,), [pl.BlockSpec((bm, K), row), pl.BlockSpec(memory_space=pl.ANY), o],
         [(o, shape((T, D), BF16))], 2 * T * K * D, T * K * 2, gather=gather,
+        scratch=[pltpu.VMEM((K, D), BF16), pltpu.SemaphoreType.DMA((n,))],
     )(p, w, h)
 
 
@@ -357,23 +429,45 @@
 
 
 def started(s):
-    oa, ob, la, lb, ra, rb, own = s
-    return (sent(oa, RIGHT), sent(ob, LEFT), sent(rb, RIGHT), sent(la, LEFT), ra, lb, own)
-
-
-def joined(s, *before):
-    from_left, from_right, far_l, far_r, ra, lb, own, *_ = lax.optimization_barrier((*s, *before))
-    to_right = (ra.astype(F32) + from_left.astype(F32)).astype(BF16)
-    to_left = (lb.astype(F32) + from_right.astype(F32)).astype(BF16)
-    return (to_right, to_left), (sent(to_right, RIGHT), sent(to_left, LEFT), far_l, far_r, own)
-
-
-def ended(s, *before):
-    near_l, near_r, far_l, far_r, own, *_ = lax.optimization_barrier((*s, *before))
-    h = own.shape[0] // 2
-    top = own[:h].astype(F32) + near_l.astype(F32) + far_r.astype(F32)
-    low = own[h:].astype(F32) + far_l.astype(F32) + near_r.astype(F32)
-    return jnp.concatenate([top, low]).astype(BF16)
+    oa, ob, la, lb, ra, rb, top, low = s
+    got = [sent(oa, RIGHT), sent(ob, LEFT), sent(rb, RIGHT), sent(la, LEFT)]
+    return (*got, ra, lb, top, low)
+
+
+def joins(s):
+    from_left, from_right, _, _, ra, lb, _, _ = s
+    return [(ra, from_left), (lb, from_right)]
+
+
+def on(s, to_right, to_left):
+    _, _, far_l, far_r, _, _, top, low = s
+    near_l, near_r = sent(to_right, RIGHT), sent(to_left, LEFT)
+    return [(top, near_l, far_r), (low, far_l, near_r)]
+
+
+def ended(sums):
+    h, c = sums[0][0].shape
+    terms = [t for group in sums for t in group]
+
+    def body(*refs):
+        at = 0
+        for i, group in enumerate(sums):
+            total = refs[at][...].astype(F32)
+            for t in refs[at + 1:at + len(group)]:
+                total = total + t[...].astype(F32)
+            refs[-1][i // 2, i % 2 * h:(i % 2 + 1) * h, :] = total.astype(BF16)
+            at += len(group)
+
+    col = c // 4
+    return call(
+        body, (4,), [pl.BlockSpec((h, col), lambda j: (0, j))] * len(terms),
+        [(pl.BlockSpec((len(sums) // 2, 2 * h, col), lambda j: (0, 0, j)), shape((len(sums) // 2, 2 * h, c), BF16))], h * c * 8, h * c * 24,
+    )(*terms)
+
+
+def summed(sums):
+    n = sum(t.size for terms in sums for t in terms)
+    return call(lambda *refs: None, (4,), [], [], n, n * 4, sums=sums)()
 
 
 PARTS = (2560, 2304, 1280)
@@ -409,40 +503,35 @@
         xu = sent(pu, ACROSS)
         sg = by_rows(at1, after(dg, pu), 1, xg)
         rg = started(sg)
-        jd, rd = joined(rd, *sg)
-        su = by_rows(at1, after(du, *jd), 1, xu)
+        *su, jr, jl = by_rows(at1, after(du, *sg), 1, xu, sums=joins(rd))
         ru = started(su)
-        part = dnormed(after(dg, *su), wgs, du, wus, h1, dy, 0, 4, ())
-        jg, rg = joined(rg, part)
-        dwd1 = ended(rd, part)
-        d1 = dnormed(after(dg, part, dwd1, *jg), wgs, du, wus, h1, dy, 4, 4, (part,))
-        ju, ru = joined(ru, d1)
-        d1 = after(d1, *ju)
-        pd = by_blocks(theirs, act0, d1)
+        ed = on(rd, jr, jl)
+        d1 = dnormed(after(dg, *su), wgs, du, wus, h1, dy, 0, 8, ())
+        pd, gr, gl, ur, ul, *dwd1 = by_blocks(theirs, act0, d1, sums=[*joins(rg), *joins(ru), *ed])
         xd = sent(pd, ACROSS)
-        dwg1 = ended(rg, pd)
-
-        du, dg = dproduct(after(d1, pd, dwg1), wd0, u0, g0)
-        dwu1 = ended(ru, dg)
-        sd = by_blocks(mine, act0, after(d1, dg, dwu1), xd)
+        eg, eu = on(rg, gr, gl), on(ru, ur, ul)
+
+        du, dg = dproduct(after(d1, pd), wd0, u0, g0)
+        *sd, gt, gb, ut, ub = by_blocks(mine, act0, after(d1, dg), xd, sums=[*eg, *eu])
         rd = started(sd)
         pg = by_rows(at0, after(dg, *sd), 0)
         xg = sent(pg, ACROSS)
         pu = by_rows(at0, after(du, pg), 0)
         xu = sent(pu, ACROSS)
-        jd, rd = joined(rd, pu)
-        sg = by_rows(at0, after(dg, *jd), 1, xg)
+        *sg, jr, jl = by_rows(at0, after(dg, pu), 1, xg, sums=joins(rd))
         rg = started(sg)
+        ed = on(rd, jr, jl)
         su = by_rows(at0, after(du, *sg), 1, xu)
         ru = started(su)
-        dwd0 = ended(rd, *su)
-        dwd = jnp.stack([dwd0, dwd1])
-        part = dnormed(after(dg, dwd, *su), [wg0], du, [wu0], h0, d1, 0, 5, ())
-        jg, rg = joined(rg, part)
-        ju, ru = joined(ru, part)
-        d0 = dnormed(after(dg, part, *jg, *ju), [wg0], du, [wu0], h0, d1, 5, 3, (part,))
-        dwg0, dwu0 = ended(rg, d0), ended(ru, d0)
-        return d0[None], jnp.stack([dwg0, dwg1]), jnp.stack([dwu0, dwu1]), dwd
+        part = dnormed(after(dg, *su), [wg0], du, [wu0], h0, d1, 0, 6, ())
+        _, jg, ju = lax.optimization_barrier((part, joins(rg), joins(ru)))
+        sums = summed([*jg, *ju])
+        g2, u2 = sums[:2], sums[2:]
+        eg, eu = on(rg, *g2), on(ru, *u2)
+        d0, *dwd0 = dnormed(after(dg, part, *g2, *u2), [wg0], du, [wu0], h0, d1, 6, 2, (part,), sums=ed)
+        dwd = jnp.stack([jnp.concatenate(dwd0), jnp.concatenate(dwd1)])
+        dwg, dwu = ended([*eg, (gt,), (gb,)]), ended([*eu, (ut,), (ub,)])
+        return d0[None], dwg, dwu, dwd
 
     data, rows = P(("rep", "dp"), None, None), P(None, "dp", None)
     out = P("rep", "dp", None)

time: 1070 us -> 1040 us (0.972)
  other arithmetic: 48.8 us -> 4.92 us
    convert_element_type x12 -> x0, other arithmetic: 26 us -> none  [the longest x6 13.7 us: joined(): to_left = (lb.astype(F32) + from_right.astype(F32)).astype(BF16)]
    concatenate x5 -> x0, other arithmetic: 17.3 us -> none  [ended(): return jnp.concatenate([top, low]).astype(BF16)]
    pallas_call x24 -> x26, Pallas kernels: 866 us -> 866 us  [run(): got = made(*args, *kept, *added, *(u[0] for u in units))]
  transfers between devices with their start and end apart: 42 -> 42, of which waited for: 10 -> 9; matrix products, arithmetic and copies ran while one was open for 3% -> 0% of each run, Pallas kernels for 35% -> 34%
where the time goes in v2:
time: 1040 us; the launch traced here: 1030 us
  Pallas kernels  866 us (83%)
  waiting for transfers between devices  115 us (11%)
  starting transfers between devices  37.8 us (4%)
    pallas_call x26, Pallas kernels, run(): got = made(*args, *kept, *added, *(u[0] for u in units))  866 us
    ppermute x42, waiting for transfers between devices, sent(): return lax.ppermute(t, 'dp', pairs)  115 us
    ppermute x42, starting transfers between devices, sent(): return lax.ppermute(t, 'dp', pairs)  37.8 us
  transfers between devices with their start and end apart: 42, of which 9 were waited for; matrix products, arithmetic and copies ran while one was open for 0% of the time, Pallas kernels for 34%

profile of v2, /device:TPU:0, one launch (start us, length us, event | category | flops | bytes accessed | tf_op | source)
XLA Modules:
  0.0 1029.1 jit_solution(14583359055881327780)
XLA Ops:
  0.6 112.4 %shard_map.93 = (bf16[2048,1024]{1,0:T(8,128)(2,1)}, bf16[1024,2048]{1,0:T(8,128)(2,1)}, bf16[1024,6144]{1,0:T(8,128)(2,1)}, bf16[1024,6144]{1,0:T(8,128)(2,1)}) custom-call(bf16[2048,1024]{1,0:T(8,128)(2,1)} %bitcast.11, bf16[2,128,6144]{2,1,0:T(8,128)(2,1)} %refs_8_.1, bf16[2,128,6144]{2,1,0:T(8,128)(2,1)} %refs_9_.1), custom_call_target="tpu_custom_call" | custom-call | flops 16777216 | bytes 12582912 | tf_op jit(solution)/shard_map/pallas_call | solution.py:169
  113.1 103.7 %shard_map.94 = (bf16[2048,6144]{1,0:T(8,128)(2,1)}, f32[2048,6144]{1,0:T(8,128)}, f32[2048,6144]{1,0:T(8,128)}, bf16[6144,1024]{1,0:T(8,128)(2,1)}, bf16[1024,2...) custom-call(bf16[2048,1024]{1,0:T(8,128)(2,1)} %get-tuple-element.125.refs_0_, ...), custom_call_target="tpu_custom_call" | custom-call | flops 51539607552 | bytes 125829120 | tf_op jit(solution)/shard_map/pallas_call | solution.py:169
  216.8 62.0 %shard_map.95 = (bf16[2048,1024]{1,0:T(8,128)(2,1)}, bf16[6144,1024]{1,0:T(8,128)(2,1)}) custom-call(bf16[2048,6144]{1,0:T(8,128)(2,1)} %get-tuple-element.128.refs_0_.refs_1_, bf16[6144,1024]{1,0:T(8,128)(2,1)} %get-tuple-element.129.refs_1_, bf16[2048,1024]{1,0:T(8,128)(2,1)} %bitcast.12, bf16[2,768,1024]{2,1,0:T(8,128)(2,1)} %refs_3_.3), custom_call_target="tpu_custom_call" | custom-call | flops 25769803776 | bytes 25165824 | tf_op jit(solution)/shard_map/pallas_call | solution.py:169
  288.5 52.5 %shard_map.97 = (bf16[2048,6144]{1,0:T(8,128)(2,1)}, bf16[2048,6144]{1,0:T(8,128)(2,1)}, bf16[2048,6144]{1,0:T(8,128)(2,1)}, bf16[1024,2304]{1,0:T(8,128)(2,1)}, bf16[1024,2304]{1,0:T(8,128)(2,1)}) custom-call(bf16[2048,1024]{1,0:T(8,128)(2,1)} %get-tuple-element.131.refs_0_, bf16[2048,1024]{1,0:T(8,128)(2,1)} %bitcast.15, ...), custom_call_target="tpu_custom_call" | custom-call | flops 32212254720 | bytes 31457280 | tf_op jit(solution)/shard_map/pallas_call | solution.py:169
  341.0 43.6 %shard_map.98 = (bf16[2048,6144]{1,0:T(8,128)(2,1)}, bf16[2048,6144]{1,0:T(8,128)(2,1)}, bf16[2048,6144]{1,0:T(8,128)(2,1)}, bf16[1024,1280]{1,0:T(8,128)(2,1)}, bf16[1024,1280]{1,0:T(8,128)(2,1)}) custom-call(bf16[2048,1024]{1,0:T(8,128)(2,1)} %get-tuple-element.131.refs_0_, ...), custom_call_target="tpu_custom_call", output_to_operand_aliasing={{0}: (5, {}), {1}: (6, {}), {2}: (7, {})} | custom-call | flops 28991029248 | bytes 28311552 | tf_op jit(solution)/shard_map/pallas_call | solution.py:169
  384.6 24.0 %shard_map.99 = (bf16[2048,6144]{1,0:T(8,128)(2,1)}, bf16[2048,6144]{1,0:T(8,128)(2,1)}, bf16[2048,6144]{1,0:T(8,128)(2,1)}) custom-call(bf16[2048,1024]{1,0:T(8,128)(2,1)} %get-tuple-element.131.refs_0_, bf16[2048,1024]{1,0:T(8,128)(2,1)} %bitcast.17, ...), custom_call_target="tpu_custom_call", output_to_operand_aliasing={{0}: (5, {}), {1}: (6, {}), {2}: (7, {})} | custom-call | flops 16106127360 | bytes 15728640 | tf_op jit(solution)/shard_map/pallas_call | solution.py:169
  408.6 19.0 %shard_map.100 = bf16[3072,1024]{1,0:T(8,128)(2,1)} custom-call(s32[4]{0:T(128)} %get-tuple-element.246.refs_0_, bf16[2048,6144]{1,0:T(8,128)(2,1)} %get-tuple-element.148.refs_1_, bf16[2048,1024]{1,0:T(8,128)(2,1)} %bitcast.18), custom_call_target="tpu_custom_call" | custom-call | flops 12884901888 | bytes 12582912 | tf_op jit(solution)/shard_map/pallas_call | solution.py:169
  427.6 18.5 %shard_map.101 = bf16[512,6144]{1,0:T(8,128)(2,1)} custom-call(bf16[1024,2048]{1,0:T(8,128)(2,1)} %get-tuple-element.146.refs_0_, bf16[2048,6144]{1,0:T(8,128)(2,1)} %get-tuple-element.178.refs_1_.refs_0_), custom_call_target="tpu_custom_call" | custom-call | flops 12884901888 | bytes 25165824 | tf_op jit(solution)/shard_map/pallas_call | solution.py:169
  446.6 21.3 %shard_map.102 = (bf16[384,1024]{1,0:T(8,128)(2,1)}, bf16[384,1024]{1,0:T(8,128)(2,1)}, bf16[384,1024]{1,0:T(8,128)(2,1)}, bf16[384,1024]{1,0:T(8,128)(2,1)}, bf...) custom-call(s32[4]{0:T(128)} %get-tuple-element.247.refs_0_, ...), custom_call_target="tpu_custom_call" | custom-call | flops 12884901888 | bytes 12582912 | tf_op jit(solution)/shard_map/pallas_call | solution.py:169
  468.0 18.5 %shard_map.103 = bf16[512,6144]{1,0:T(8,128)(2,1)} custom-call(bf16[1024,2048]{1,0:T(8,128)(2,1)} %get-tuple-element.146.refs_0_, bf16[2048,6144]{1,0:T(8,128)(2,1)} %get-tuple-element.169.refs_1_), custom_call_target="tpu_custom_call" | custom-call | flops 12884901888 | bytes 25165824 | tf_op jit(solution)/shard_map/pallas_call | solution.py:169
  488.5 19.1 %shard_map.104 = (bf16[64,6144]{1,0:T(8,128)(2,1)}, bf16[64,6144]{1,0:T(8,128)(2,1)}, bf16[64,6144]{1,0:T(8,128)(2,1)}, bf16[64,6144]{1,0:T(8,128)(2,1)}, bf16[6...) custom-call(bf16[1024,2048]{1,0:T(8,128)(2,1)} %get-tuple-element.146.refs_0, ...), custom_call_target="tpu_custom_call" | custom-call | flops 12884901888 | bytes 25165824 | tf_op jit(solution)/shard_map/pallas_call | solution.py:169
  511.7 20.4 %shard_map.105 = (bf16[64,6144]{1,0:T(8,128)(2,1)}, bf16[64,6144]{1,0:T(8,128)(2,1)}, bf16[64,6144]{1,0:T(8,128)(2,1)}, bf16[64,6144]{1,0:T(8,128)(2,1)}, bf16[6...) custom-call(bf16[1024,2048]{1,0:T(8,128)(2,1)} %get-tuple-element.14, ...), custom_call_target="tpu_custom_call" | custom-call | flops 12884901888 | bytes 25165824 | tf_op jit(solution)/shard_map/pallas_call | solution.py:169
  547.2 66.2 %shard_map.106.refs_2_.refs_0_.refs_5_ = bf16[2048,1024]{1,0:T(8,128)(2,1)} custom-call(bf16[2048,6144]{1,0:T(8,128)(2,1)} %get-tuple-element.178.refs_1_.refs_0_, bf16[2048,6144]{1,0:T(8,128)(2,1)} %get-tuple-element.169.refs_1_, bf16[1024,2560]{1,0:T(8,128)(2,1)} %get-tuple-element.132.refs_2_, bf16[1024,2304]{1,0:T(8,128)(2,1)} %get-tuple-element.135.refs_2_.refs_3_, ...), custom_call_target="tpu_custom_call" | custom-call | flops 51539607552 | bytes 50331648 | tf_op jit(solution)/shard_map/pallas_call | solution.py:169
  613.5 22.1 %shard_map.107 = (bf16[3072,1024]{1,0:T(8,128)(2,1)}, bf16[64,6144]{1,0:T(8,128)(2,1)}, bf16[64,6144]{1,0:T(8,128)(2,1)}, bf16[64,6144]{1,0:T(8,128)(2,1)}, bf16...) custom-call(s32[4]{0:T(128)} %get-tuple-element.246.refs_0_, ...), custom_call_target="tpu_custom_call" | custom-call | flops 12884901888 | bytes 12582912 | tf_op jit(solution)/shard_map/pallas_call | solution.py:169
  639.7 16.4 %collective-permute-done.15.refs_6_ = bf16[64,6144]{1,0:T(8,128)(2,1)S(1)} collective-permute-done((bf16[64,6144]{1,0:T(8,128)(2,1)S(1)}, bf16[64,6144]{1,0:T(8,128)(2,1)S(1)}, u32[]{:S(2)}, u32[]{:S(2)}) %collective-permute-start.15) | collective-permute-done | bytes 786464 | tf_op jit(solution)/shard_map/ppermute | solution.py:239
  675.1 61.6 %shard_map.108 = (bf16[2048,6144]{1,0:T(8,128)(2,1)}, bf16[2048,6144]{1,0:T(8,128)(2,1)}) custom-call(bf16[2048,1024]{1,0:T(8,128)(2,1)} %shard_map.106.refs_2_.refs_0_.refs_5_, bf16[6144,1024]{1,0:T(8,128)(2,1)} %get-tuple-element.129.refs_1_, f32[2048,6144]{1,0:T(8,128)} %get-tuple-element.183.refs_2_, f32[2048,6144]{1,0:T(8,128)} %get-tuple-element.184.refs_3_), custom_call_target="tpu_custom_call" | custom-call | flops 25769803776 | bytes 150994944 | tf_op jit(solution)/shard_map/pallas_call | solution.py:169
  737.8 24.5 %shard_map.109 = (bf16[384,1024]{1,0:T(8,128)(2,1)}, bf16[384,1024]{1,0:T(8,128)(2,1)}, bf16[384,1024]{1,0:T(8,128)(2,1)}, bf16[384,1024]{1,0:T(8,128)(2,1)}, bf...) custom-call(s32[4]{0:T(128)} %get-tuple-element.247.refs_0_, ...), custom_call_target="tpu_custom_call" | custom-call | flops 12884901888 | bytes 12582912 | tf_op jit(solution)/shard_map/pallas_call | solution.py:169
  762.3 18.5 %shard_map.110 = bf16[512,6144]{1,0:T(8,128)(2,1)} custom-call(bf16[1024,2048]{1,0:T(8,128)(2,1)} %get-tuple-element.186.refs_0_, bf16[2048,6144]{1,0:T(8,128)(2,1)} %get-tuple-element.234.refs_1_.refs_0_), custom_call_target="tpu_custom_call" | custom-call | flops 12884901888 | bytes 25165824 | tf_op jit(solution)/shard_map/pallas_call | solution.py:169
  780.8 18.6 %shard_map.111 = bf16[512,6144]{1,0:T(8,128)(2,1)} custom-call(bf16[1024,2048]{1,0:T(8,128)(2,1)} %get-tuple-element.186.refs_0_, bf16[2048,6144]{1,0:T(8,128)(2,1)} %get-tuple-element.212.refs_1_), custom_call_target="tpu_custom_call" | custom-call | flops 12884901888 | bytes 25165824 | tf_op jit(solution)/shard_map/pallas_call | solution.py:169
  802.0 17.4 %collective-permute-done.23.refs_4_ = bf16[384,1024]{1,0:T(8,128)(2,1)S(1)} collective-permute-done((bf16[384,1024]{1,0:T(8,128)(2,1)S(1)}, bf16[384,1024]{1,0:T(8,128)(2,1)S(1)}, u32[]{:S(2)}, u32[]{:S(2)}) %collective-permute-start.23) | collective-permute-done | bytes 786464 | tf_op jit(solution)/shard_map/ppermute | solution.py:239
  821.2 20.3 %shard_map.112 = (bf16[64,6144]{1,0:T(8,128)(2,1)}, bf16[64,6144]{1,0:T(8,128)(2,1)}, bf16[64,6144]{1,0:T(8,128)(2,1)}, bf16[64,6144]{1,0:T(8,128)(2,1)}, bf16[6...) custom-call(bf16[1024,2048]{1,0:T(8,128)(2,1)} %get-tuple-element.18, ...), custom_call_target="tpu_custom_call" | custom-call | flops 12884901888 | bytes 25165824 | tf_op jit(solution)/shard_map/pallas_call | solution.py:169
  841.5 19.1 %shard_map.113 = (bf16[64,6144]{1,0:T(8,128)(2,1)}, bf16[64,6144]{1,0:T(8,128)(2,1)}, bf16[64,6144]{1,0:T(8,128)(2,1)}, bf16[64,6144]{1,0:T(8,128)(2,1)}, bf16[6...) custom-call(bf16[1024,2048]{1,0:T(8,128)(2,1)} %get-tuple-element.186.refs_0, ...), custom_call_target="tpu_custom_call" | custom-call | flops 12884901888 | bytes 25165824 | tf_op jit(solution)/shard_map/pallas_call | solution.py:169
  882.3 51.6 %shard_map.114.refs_6_ = bf16[2048,1024]{1,0:T(8,128)(2,1)} custom-call(bf16[2048,6144]{1,0:T(8,128)(2,1)} %get-tuple-element.234.refs_1_.refs_0_, bf16[2048,6144]{1,0:T(8,128)(2,1)} %get-tuple-element.212.refs_1_, bf16[1024,6144]{1,0:T(8,128)(2,1)} %get-tuple-element.126.refs_1_.refs_2_, bf16[1024,6144]{1,0:T(8,128)(2,1)} %get-tuple-element.127.refs_2_.refs_3_, ...), custom_call_target="tpu_custom_call" | custom-call | flops 38654705664 | bytes 37748736 | tf_op jit(solution)/shard_map/pallas_call | solution.py:169
  990.4 24.8 %shard_map.116 = (bf16[2048,1024]{1,0:T(8,128)(2,1)}, bf16[384,1024]{1,0:T(8,128)(2,1)}, bf16[384,1024]{1,0:T(8,128)(2,1)}) custom-call(bf16[2048,6144]{1,0:T(8,128)(2,1)} %get-tuple-element.234.refs_1_.refs_0_, bf16[2048,6144]{1,0:T(8,128)(2,1)} %get-tuple-element.212.refs_1_, ...), custom_call_target="tpu_custom_call", output_to_operand_aliasing={{0}: (6, {})} | custom-call | flops 12884901888 | bytes 12582912 | tf_op jit(solution)/shard_map/pallas_call | solution.py:169
  (119 shorter events, 151.9 us)
Async XLA Ops:
  446.1 42.4 %collective-permute-start.1 = (bf16[512,6144]{1,0:T(8,128)(2,1)}, bf16[512,6144]{1,0:T(8,128)(2,1)}, u32[]{:S(2)}, u32[]{:S(2)}) collective-permute-start(bf16[512,6144]{1,0:T(8,128)(2,1)} %shard_map.101), channel_id=1, source_target_pairs={{0,1},{1,0},{2,3},{3,2},{4,5},{5,4},{6,7},{7,6}} | collective-permute-start | bytes 18874376 | tf_op jit(solution)/shard_map/ppermute | solution.py:239
  510.7 102.8 %collective-permute-start.11 = (bf16[384,1024]{1,0:T(8,128)(2,1)}, bf16[384,1024]{1,0:T(8,128)(2,1)}, u32[]{:S(2)}, u32[]{:S(2)}) collective-permute-start(bf16[384,1024]{1,0:T(8,128)(2,1)} %get-tuple-element.156), channel_id=1, source_target_pairs={{0,2},{1,3},{2,6},{3,7},{4,0},{5,1},{6,4},{7,5}} | collective-permute-start | bytes 2359304 | tf_op jit(solution)/shard_map/ppermute | solution.py:239
  532.0 81.5 %collective-permute-start.7 = (bf16[64,6144]{1,0:T(8,128)(2,1)}, bf16[64,6144]{1,0:T(8,128)(2,1)}, u32[]{:S(2)}, u32[]{:S(2)}) collective-permute-start(bf16[64,6144]{1,0:T(8,128)(2,1)} %get-tuple-element.170), channel_id=1, source_target_pairs={{0,2},{1,3},{2,6},{3,7},{4,0},{5,1},{6,4},{7,5}} | collective-permute-start | bytes 2359304 | tf_op jit(solution)/shard_map/ppermute | solution.py:239
  533.1 80.4 %collective-permute-start.8 = (bf16[64,6144]{1,0:T(8,128)(2,1)}, bf16[64,6144]{1,0:T(8,128)(2,1)}, u32[]{:S(2)}, u32[]{:S(2)}) collective-permute-start(bf16[64,6144]{1,0:T(8,128)(2,1)} %get-tuple-element.171), channel_id=1, source_target_pairs={{0,4},{1,5},{2,0},{3,1},{4,6},{5,7},{6,2},{7,3}} | collective-permute-start | bytes 2359304 | tf_op jit(solution)/shard_map/ppermute | solution.py:239
  534.1 79.4 %collective-permute-start.12 = (bf16[384,1024]{1,0:T(8,128)(2,1)}, bf16[384,1024]{1,0:T(8,128)(2,1)}, u32[]{:S(2)}, u32[]{:S(2)}) collective-permute-start(bf16[384,1024]{1,0:T(8,128)(2,1)} %get-tuple-element.180), channel_id=1, source_target_pairs={{0,4},{1,5},{2,0},{3,1},{4,6},{5,7},{6,2},{7,3}} | collective-permute-start | bytes 2359304 | tf_op jit(solution)/shard_map/ppermute | solution.py:239
  546.3 67.3 %collective-permute-start.9 = (bf16[384,1024]{1,0:T(8,128)(2,1)}, bf16[384,1024]{1,0:T(8,128)(2,1)}, u32[]{:S(2)}, u32[]{:S(2)}) collective-permute-start(bf16[384,1024]{1,0:T(8,128)(2,1)} %get-tuple-element.179), channel_id=1, source_target_pairs={{0,2},{1,3},{2,6},{3,7},{4,0},{5,1},{6,4},{7,5}} | collective-permute-start | bytes 2359304 | tf_op jit(solution)/shard_map/ppermute | solution.py:239
  635.6 101.1 %collective-permute-start.13 = (bf16[3072,1024]{1,0:T(8,128)(2,1)}, bf16[3072,1024]{1,0:T(8,128)(2,1)}, u32[]{:S(2)}, u32[]{:S(2)}) collective-permute-start(bf16[3072,1024]{1,0:T(8,128)(2,1)} %get-tuple-element.181), channel_id=1, source_target_pairs={{0,1},{1,0},{2,3},{3,2},{4,5},{5,4},{6,7},{7,6}} | collective-permute-start | bytes 18874376 | tf_op jit(solution)/shard_map/ppermute | solution.py:239
  656.1 80.6 %collective-permute-start.14 = (bf16[64,6144]{1,0:T(8,128)(2,1)}, bf16[64,6144]{1,0:T(8,128)(2,1)S(1)}, u32[]{:S(2)}, u32[]{:S(2)}) collective-permute-start(bf16[64,6144]{1,0:T(8,128)(2,1)} %get-tuple-element.189), channel_id=1, source_target_pairs={{0,2},{1,3},{2,6},{3,7},{4,0},{5,1},{6,4},{7,5}} | collective-permute-start | bytes 2359304 | tf_op jit(solution)/shard_map/ppermute | solution.py:239
  658.0 78.7 %collective-permute-start.17 = (bf16[64,6144]{1,0:T(8,128)(2,1)}, bf16[64,6144]{1,0:T(8,128)(2,1)S(1)}, u32[]{:S(2)}, u32[]{:S(2)}) collective-permute-start(bf16[64,6144]{1,0:T(8,128)(2,1)} %get-tuple-element.190), channel_id=1, source_target_pairs={{0,4},{1,5},{2,0},{3,1},{4,6},{5,7},{6,2},{7,3}} | collective-permute-start | bytes 2359304 | tf_op jit(solution)/shard_map/ppermute | solution.py:239
  673.1 63.7 %collective-permute-start.18 = (bf16[64,6144]{1,0:T(8,128)(2,1)}, bf16[64,6144]{1,0:T(8,128)(2,1)}, u32[]{:S(2)}, u32[]{:S(2)}) collective-permute-start(bf16[64,6144]{1,0:T(8,128)(2,1)} %get-tuple-element.191), channel_id=1, source_target_pairs={{0,2},{1,3},{2,6},{3,7},{4,0},{5,1},{6,4},{7,5}} | collective-permute-start | bytes 2359304 | tf_op jit(solution)/shard_map/ppermute | solution.py:239
  674.1 62.6 %collective-permute-start.21 = (bf16[64,6144]{1,0:T(8,128)(2,1)}, bf16[64,6144]{1,0:T(8,128)(2,1)}, u32[]{:S(2)}, u32[]{:S(2)}) collective-permute-start(bf16[64,6144]{1,0:T(8,128)(2,1)} %get-tuple-element.192), channel_id=1, source_target_pairs={{0,4},{1,5},{2,0},{3,1},{4,6},{5,7},{6,2},{7,3}} | collective-permute-start | bytes 2359304 | tf_op jit(solution)/shard_map/ppermute | solution.py:239
  780.8 40.3 %collective-permute-start.22 = (bf16[512,6144]{1,0:T(8,128)(2,1)}, bf16[512,6144]{1,0:T(8,128)(2,1)}, u32[]{:S(2)}, u32[]{:S(2)}) collective-permute-start(bf16[512,6144]{1,0:T(8,128)(2,1)} %shard_map.110), channel_id=1, source_target_pairs={{0,1},{1,0},{2,3},{3,2},{4,5},{5,4},{6,7},{7,6}} | collective-permute-start | bytes 18874376 | tf_op jit(solution)/shard_map/ppermute | solution.py:239
  799.4 42.0 %collective-permute-start.25 = (bf16[512,6144]{1,0:T(8,128)(2,1)}, bf16[512,6144]{1,0:T(8,128)(2,1)}, u32[]{:S(2)}, u32[]{:S(2)}) collective-permute-start(bf16[512,6144]{1,0:T(8,128)(2,1)} %shard_map.111), channel_id=1, source_target_pairs={{0,1},{1,0},{2,3},{3,2},{4,5},{5,4},{6,7},{7,6}} | collective-permute-start | bytes 18874376 | tf_op jit(solution)/shard_map/ppermute | solution.py:239
  861.6 80.4 %collective-permute-start.31 = (bf16[384,1024]{1,0:T(8,128)(2,1)}, bf16[384,1024]{1,0:T(8,128)(2,1)S(1)}, u32[]{:S(2)}, u32[]{:S(2)}) collective-permute-start(bf16[384,1024]{1,0:T(8,128)(2,1)} %get-tuple-element.195), channel_id=1, source_target_pairs={{0,4},{1,5},{2,0},{3,1},{4,6},{5,7},{6,2},{7,3}} | collective-permute-start | bytes 2359304 | tf_op jit(solution)/shard_map/ppermute | solution.py:239
  862.6 80.6 %collective-permute-start.32 = (bf16[384,1024]{1,0:T(8,128)(2,1)}, bf16[384,1024]{1,0:T(8,128)(2,1)S(1)}, u32[]{:S(2)}, u32[]{:S(2)}) collective-permute-start(bf16[384,1024]{1,0:T(8,128)(2,1)} %get-tuple-element.198), channel_id=1, source_target_pairs={{0,2},{1,3},{2,6},{3,7},{4,0},{5,1},{6,4},{7,5}} | collective-permute-start | bytes 2359304 | tf_op jit(solution)/shard_map/ppermute | solution.py:239
  863.6 71.3 %collective-permute-start.26 = (bf16[64,6144]{1,0:T(8,128)(2,1)}, bf16[64,6144]{1,0:T(8,128)(2,1)}, u32[]{:S(2)}, u32[]{:S(2)}) collective-permute-start(bf16[64,6144]{1,0:T(8,128)(2,1)} %get-tuple-element.204), channel_id=1, source_target_pairs={{0,2},{1,3},{2,6},{3,7},{4,0},{5,1},{6,4},{7,5}} | collective-permute-start | bytes 2359304 | tf_op jit(solution)/shard_map/ppermute | solution.py:239
  864.6 69.4 %collective-permute-start.29 = (bf16[64,6144]{1,0:T(8,128)(2,1)}, bf16[64,6144]{1,0:T(8,128)(2,1)}, u32[]{:S(2)}, u32[]{:S(2)}) collective-permute-start(bf16[64,6144]{1,0:T(8,128)(2,1)} %get-tuple-element.214), channel_id=1, source_target_pairs={{0,4},{1,5},{2,0},{3,1},{4,6},{5,7},{6,2},{7,3}} | collective-permute-start | bytes 2359304 | tf_op jit(solution)/shard_map/ppermute | solution.py:239
  881.3 54.7 %collective-permute-start.27 = (bf16[64,6144]{1,0:T(8,128)(2,1)}, bf16[64,6144]{1,0:T(8,128)(2,1)}, u32[]{:S(2)}, u32[]{:S(2)}) collective-permute-start(bf16[64,6144]{1,0:T(8,128)(2,1)} %get-tuple-element.205), channel_id=1, source_target_pairs={{0,4},{1,5},{2,0},{3,1},{4,6},{5,7},{6,2},{7,3}} | collective-permute-start | bytes 2359304 | tf_op jit(solution)/shard_map/ppermute | solution.py:239
  934.0 38.6 %collective-permute-start.39 = (bf16[64,6144]{1,0:T(8,128)(2,1)}, bf16[64,6144]{1,0:T(8,128)(2,1)}, u32[]{:S(2)}, u32[]{:S(2)}) collective-permute-start(bf16[64,6144]{1,0:T(8,128)(2,1)} %get-tuple-element.215), channel_id=1, source_target_pairs={{0,4},{1,5},{2,0},{3,1},{4,6},{5,7},{6,2},{7,3}} | collective-permute-start | bytes 2359304 | tf_op jit(solution)/shard_map/ppermute | solution.py:239
  943.1 46.2 %collective-permute-start.38 = (bf16[64,6144]{1,0:T(8,128)(2,1)}, bf16[64,6144]{1,0:T(8,128)(2,1)}, u32[]{:S(2)}, u32[]{:S(2)}) collective-permute-start(bf16[64,6144]{1,0:T(8,128)(2,1)} %get-tuple-element.232), channel_id=1, source_target_pairs={{0,2},{1,3},{2,6},{3,7},{4,0},{5,1},{6,4},{7,5}} | collective-permute-start | bytes 2359304 | tf_op jit(solution)/shard_map/ppermute | solution.py:239
  955.7 68.1 %collective-permute-start.35 = (bf16[64,6144]{1,0:T(8,128)(2,1)}, bf16[64,6144]{1,0:T(8,128)(2,1)}, u32[]{:S(2)}, u32[]{:S(2)}) collective-permute-start(bf16[64,6144]{1,0:T(8,128)(2,1)} %get-tuple-element.206), channel_id=1, source_target_pairs={{0,4},{1,5},{2,0},{3,1},{4,6},{5,7},{6,2},{7,3}} | collective-permute-start | bytes 2359304 | tf_op jit(solution)/shard_map/ppermute | solution.py:239
  971.6 52.2 %collective-permute-start.36 = (bf16[64,6144]{1,0:T(8,128)(2,1)}, bf16[64,6144]{1,0:T(8,128)(2,1)}, u32[]{:S(2)}, u32[]{:S(2)}) collective-permute-start(bf16[64,6144]{1,0:T(8,128)(2,1)} %get-tuple-element.209), channel_id=1, source_target_pairs={{0,2},{1,3},{2,6},{3,7},{4,0},{5,1},{6,4},{7,5}} | collective-permute-start | bytes 2359304 | tf_op jit(solution)/shard_map/ppermute | solution.py:239
  972.6 46.1 %collective-permute-start.41 = (bf16[64,6144]{1,0:T(8,128)(2,1)}, bf16[64,6144]{1,0:T(8,128)(2,1)}, u32[]{:S(2)}, u32[]{:S(2)}) collective-permute-start(bf16[64,6144]{1,0:T(8,128)(2,1)} %get-tuple-element.233), channel_id=1, source_target_pairs={{0,4},{1,5},{2,0},{3,1},{4,6},{5,7},{6,2},{7,3}} | collective-permute-start | bytes 2359304 | tf_op jit(solution)/shard_map/ppermute | solution.py:239
  973.6 50.2 %collective-permute-start.34 = (bf16[64,6144]{1,0:T(8,128)(2,1)}, bf16[64,6144]{1,0:T(8,128)(2,1)}, u32[]{:S(2)}, u32[]{:S(2)}) collective-permute-start(bf16[64,6144]{1,0:T(8,128)(2,1)} %get-tuple-element.230), channel_id=1, source_target_pairs={{0,2},{1,3},{2,6},{3,7},{4,0},{5,1},{6,4},{7,5}} | collective-permute-start | bytes 2359304 | tf_op jit(solution)/shard_map/ppermute | solution.py:239
  (32 other events, 592.1 us)

commit v3 on v2

--- a/solution.py
+++ b/solution.py
@@ -66,6 +66,10 @@
         self.number, self.units, self.ticks = number, units, ticks
 
 
+def plane_of(t):
+    return t if isinstance(t, tuple) else (t, None)
+
+
 def call(body, grid, ins, outs, flops, nbytes, prefetch=0, gather=None, kept=(), scratch=(), sums=(), vmem=62 * 2**20):
     n_in, n_out, n_kept, n_main = prefetch + len(ins), len(outs), len(kept), len(outs)
     added = [t for terms in sums for t in terms]
@@ -134,10 +138,13 @@
         steps = grid[0]
 
         def piece(t):
-            r, c = t.shape
-            if c % (128 * steps) == 0:
-                return pl.BlockSpec((r, c // steps), lambda j, *_: (0, j))
-            return pl.BlockSpec((r // steps, c), lambda j, *_: (j, 0))
+            whole, plane = plane_of(t)
+            r, c = whole.shape[-2:]
+            across = c % (128 * steps) == 0
+            block = (r, c // steps) if across else (r // steps, c)
+            if plane is None:
+                return pl.BlockSpec(block, lambda j, *_: (0, j) if across else (j, 0))
+            return pl.BlockSpec((None, *block), lambda j, *_: (plane, 0, j) if across else (plane, j, 0))
 
         specs += [piece(t) for t in added]
         outs = list(outs) + [(piece(terms[0]), shape(terms[0].shape, BF16)) for terms in sums]
@@ -166,14 +173,26 @@
     )
 
     def run(*args):
-        got = made(*args, *kept, *added, *(u[0] for u in units))
+        got = made(*args, *kept, *(plane_of(t)[0] for t in added), *(u[0] for u in units))
         return got[0] if len(outs) == 1 else got
 
     return run
 
 
+PIECES = ((0, 5), (1, 2), (4,), (3,), (6,), (7,))
+
+
 def pieces(rows, cols):
-    return [(rows // 8, cols)] * 8
+    return [(len(p), rows // 8, cols) if len(p) > 1 else (rows // 8, cols) for p in PIECES]
+
+
+def put(outs, half, value):
+    for o_ref, p in zip(outs, PIECES):
+        if half in p:
+            if len(p) > 1:
+                o_ref[p.index(half)] = value
+            else:
+                o_ref[...] = value
 
 
 def by_rows(at, d, half, got=None, bn=1024, sums=()):
@@ -187,7 +206,7 @@
     def mine(a_ref, d_ref, got_ref, *outs):
         t = (dot(a_ref[...], d_ref[...], NN) + got_ref[...].astype(F32)).astype(BF16)
         for i in range(8):
-            outs[i][...] = t[i * h:(i + 1) * h, :]
+            put(outs, i, t[i * h:(i + 1) * h, :])
 
     col = lambda j: (0, j)
     ins = [pl.BlockSpec((rows, T), lambda j: (half, 0), pipeline_mode=ONE), pl.BlockSpec((T, bn), col)]
@@ -196,7 +215,7 @@
         ins.append(pl.BlockSpec((rows, bn), col))
         args.append(got)
         results = pieces(rows, N)
-    outs = [(pl.BlockSpec((r, bn), col), shape((r, N), BF16)) for r, _ in results]
+    outs = [(pl.BlockSpec((*s[:-1], bn), functools.partial(lambda k, j: (0,) * k + (j,), len(s) - 1)), shape(s, BF16)) for s in results]
     return call(theirs if got is None else mine, (N // bn,), ins, outs, 2 * rows * T * N, T * N * 2, sums=sums)(*args)
 
 
@@ -218,8 +237,8 @@
         for i in range(4):
             @pl.when(step == i)
             def _():
-                outs[2 * i][...] = refs[parts + 1][:h, :]
-                outs[2 * i + 1][...] = refs[parts + 1][h:, :]
+                put(outs, 2 * i, refs[parts + 1][:h, :])
+                put(outs, 2 * i + 1, refs[parts + 1][h:, :])
 
     ins = [pl.BlockSpec((T, width), functools.partial(lambda c, i, o: (0, c * 8 + o[i]), c)) for c in range(parts)]
     ins.append(pl.BlockSpec((T, D), lambda i, o: (0, 0), pipeline_mode=ONE))
@@ -229,7 +248,7 @@
     if got is not None:
         ins.append(block)
         args.append(got)
-        outs = [(pl.BlockSpec(s, lambda i, o: (0, 0)), shape(s, BF16)) for s in pieces(n * bm, D)]
+        outs = [(pl.BlockSpec(s, functools.partial(lambda k, i, o: (0,) * k, len(s))), shape(s, BF16)) for s in pieces(n * bm, D)]
     return call(
         theirs if got is None else mine, (n,), ins, outs, 2 * n * bm * T * D, T * n * bm * 2, prefetch=1, sums=sums
     )(*args)
@@ -269,7 +288,7 @@
     return lambda i: copies[i].wait()
 
 
-def dproduct(dy, wd, by_u, by_g, bm=256, bn=1024):
+def dproduct(dy, wd, by_u, by_g, start, steps, kept, sums=(), bm=256, bn=1024):
     T, D = dy.shape
     N = wd.shape[0]
     n = N // bn
@@ -292,11 +311,11 @@
         def _():
             all_of(lambda i: None)
 
-    row = lambda j: (j, 0)
+    row = lambda j: (start + j, 0)
     o = pl.BlockSpec((bm, N), row)
     return call(
-        body, (T // bm,), [pl.BlockSpec((bm, D), row), pl.BlockSpec(memory_space=pl.ANY), o, o],
-        [(o, shape((T, N), BF16)), (o, shape((T, N), BF16))], 2 * T * D * N, T * N * 12,
+        body, (steps,), [pl.BlockSpec((bm, D), row), pl.BlockSpec(memory_space=pl.ANY), o, o],
+        [(o, shape((T, N), BF16)), (o, shape((T, N), BF16))], 2 * steps * bm * D * N, steps * bm * N * 12, kept=kept, sums=sums,
         scratch=[pltpu.VMEM((N, D), BF16), pltpu.SemaphoreType.DMA((n,))],
     )(dy, wd, by_u, by_g)
 
@@ -332,7 +351,7 @@
     D = wgs[0].shape[0]
     cuts, at = [], 0
     for p, w in enumerate(wgs):
-        each = next(c for c in (1280, 1152, 1024) if w.shape[1] % c == 0)
+        each = next(c for c in (1280, 1024, 768) if w.shape[1] % c == 0)
         for i in range(w.shape[1] // each):
             cuts.append((p, i * each, at + i * each, each))
         at += w.shape[1]
@@ -378,7 +397,7 @@
     D = w.shape[1]
     n = K // bk
 
-    def body(p_ref, w_hbm, h_ref, o_ref, w_ref, sems):
+    def body(p_ref, w_hbm, h_ref, o_ref, a_ref, t_ref, w_ref, sems):
         @pl.when(pl.program_id(0) == 0)
         def _():
             cuts = [pl.ds(i * bk, bk) for i in range(n)]
@@ -394,32 +413,35 @@
         def _():
             o_ref[...] = h_ref[...] + dot(p_ref[...], w_ref[...], NN).astype(BF16)
 
+        norm(o_ref, a_ref, t_ref)
+
     row = lambda i: (i, 0)
     o = pl.BlockSpec((bm, D), row)
+    s = shape((T, D), BF16)
     return call(
         body, (T // bm,), [pl.BlockSpec((bm, K), row), pl.BlockSpec(memory_space=pl.ANY), o],
-        [(o, shape((T, D), BF16))], 2 * T * K * D, T * K * 2, gather=gather,
+        [(o, s), (o, s), (pl.BlockSpec((D, bm), lambda i: (0, i)), shape((D, T), BF16))], 2 * T * K * D, T * K * 2, gather=gather,
         scratch=[pltpu.VMEM((K, D), BF16), pltpu.SemaphoreType.DMA((n,))],
     )(p, w, h)
 
 
-def normed(h, gather=None, bm=256):
+def norm(h_ref, o_ref, t_ref):
+    wide = h_ref[...].astype(F32)
+    scale = lax.rsqrt(jnp.mean(wide**2, -1, keepdims=True) + 1e-6)
+    o_ref[...] = (wide * scale).astype(BF16)
+    b = h_ref.shape[1] // 8
+    me, nxt, prv, _ = place()
+    opp = 6 - me + 2 * (me % 2)
+    for i, d in enumerate((opp, prv, nxt, me)):
+        for j, block in ((i, d + 1 - 2 * (d % 2)), (i + 4, d)):
+            t_ref[j * b:(j + 1) * b, :] = o_ref[:, pl.ds(pl.multiple_of(block * b, b), b)].T
+
+
+def normed(h, gather, bm=256):
     T, D = h.shape
-    b = D // 8
-
-    def body(h_ref, o_ref, t_ref):
-        wide = h_ref[...].astype(F32)
-        scale = lax.rsqrt(jnp.mean(wide**2, -1, keepdims=True) + 1e-6)
-        o_ref[...] = (wide * scale).astype(BF16)
-        me, nxt, prv, _ = place()
-        opp = 6 - me + 2 * (me % 2)
-        for i, d in enumerate((opp, prv, nxt, me)):
-            for j, block in ((i, d + 1 - 2 * (d % 2)), (i + 4, d)):
-                t_ref[j * b:(j + 1) * b, :] = o_ref[:, pl.ds(pl.multiple_of(block * b, b), b)].T
-
     o = pl.BlockSpec((bm, D), lambda i: (i, 0))
     return call(
-        body, (T // bm,), [o], [(o, shape((T, D), BF16)), (pl.BlockSpec((D, bm), lambda i: (0, i)), shape((D, T), BF16))],
+        norm, (T // bm,), [o], [(o, shape((T, D), BF16)), (pl.BlockSpec((D, bm), lambda i: (0, i)), shape((D, T), BF16))],
         T * D * 8, T * D * 6, gather=gather,
     )(h)
 
@@ -429,25 +451,24 @@
 
 
 def started(s):
-    oa, ob, la, lb, ra, rb, top, low = s
-    got = [sent(oa, RIGHT), sent(ob, LEFT), sent(rb, RIGHT), sent(la, LEFT)]
-    return (*got, ra, lb, top, low)
+    to_right, to_left, ra, lb, top, low = s
+    return sent(to_right, RIGHT), sent(to_left, LEFT), ra, lb, top, low
 
 
 def joins(s):
-    from_left, from_right, _, _, ra, lb, _, _ = s
-    return [(ra, from_left), (lb, from_right)]
+    from_left, from_right, ra, lb, _, _ = s
+    return [(ra, (from_left, 0)), (lb, (from_right, 0))]
 
 
 def on(s, to_right, to_left):
-    _, _, far_l, far_r, _, _, top, low = s
+    from_left, from_right, _, _, top, low = s
     near_l, near_r = sent(to_right, RIGHT), sent(to_left, LEFT)
-    return [(top, near_l, far_r), (low, far_l, near_r)]
+    return [(top, near_l, (from_right, 1)), (low, (from_left, 1), near_r)]
 
 
 def ended(sums):
     h, c = sums[0][0].shape
-    terms = [t for group in sums for t in group]
+    terms = [plane_of(t) for group in sums for t in group]
 
     def body(*refs):
         at = 0
@@ -459,18 +480,21 @@
             at += len(group)
 
     col = c // 4
-    return call(
-        body, (4,), [pl.BlockSpec((h, col), lambda j: (0, j))] * len(terms),
+    ins = [
+        pl.BlockSpec((h, col), lambda j: (0, j)) if p is None else pl.BlockSpec((None, h, col), functools.partial(lambda p, j: (p, 0, j), p))
+        for _, p in terms
+    ]
+    return call(
+        body, (4,), ins,
         [(pl.BlockSpec((len(sums) // 2, 2 * h, col), lambda j: (0, 0, j)), shape((len(sums) // 2, 2 * h, c), BF16))], h * c * 8, h * c * 24,
-    )(*terms)
+    )(*(t for t, _ in terms))
 
 
 def summed(sums):
-    n = sum(t.size for terms in sums for t in terms)
-    return call(lambda *refs: None, (4,), [], [], n, n * 4, sums=sums)()
-
-
-PARTS = (2560, 2304, 1280)
+    return call(lambda *refs: None, (4,), [], [], 1000000, 1000000, sums=sums)()
+
+
+PARTS = (2560, 2048, 1536)
 
 
 def solution(mesh):
@@ -486,10 +510,9 @@
         gu = lambda c: [(w, cols(c), (n, PARTS[c])) for w in (wg, wu)]
         a0, at0, wg0, wu0 = normed(h0, Gather(0, [(wg, first, (n, None)), (wu, first, (n, None))], [(7, 8), (7, 8)]))
         act0, u0, g0, wd0, *w1 = gateup(a0, wg0, wu0, Gather(1, [(wd, first, (own, None)), *gu(0)], [(14, 24), (20, 24), (23, 24)]))
-        h1, wd1 = down(act0, wd0, h0, Gather(2, [(wd, second, (own, None))], [(7, 8)]))
-        a1, at1 = normed(h1)
-        act1, du, dg, *w2 = both(a1, dy, *w1, wd1, offsets[0], Gather(3, gu(1), [(3, 8), (6, 10)]), ())
-        act1, du, dg, *w3 = both(a1, dy, *w2, wd1, offsets[1], Gather(4, gu(2), [(2, 5), (4, 6)]), (act1, du, dg))
+        h1, a1, at1, wd1 = down(act0, wd0, h0, Gather(2, [(wd, second, (own, None))], [(7, 8)]))
+        act1, du, dg, *w2 = both(a1, dy, *w1, wd1, offsets[0], Gather(3, gu(1), [(3, 7), (6, 8)]), ())
+        act1, du, dg, *w3 = both(a1, dy, *w2, wd1, offsets[1], Gather(4, gu(2), [(3, 5), (5, 7)]), (act1, du, dg))
         act1, du, dg = both(a1, dy, *w3, wd1, offsets[2], None, (act1, du, dg))
         wgs, wus = [w1[0], w2[0], w3[0]], [w1[1], w2[1], w3[1]]
 
@@ -511,25 +534,26 @@
         xd = sent(pd, ACROSS)
         eg, eu = on(rg, gr, gl), on(ru, ur, ul)
 
-        du, dg = dproduct(after(d1, pd), wd0, u0, g0)
+        du, dg = dproduct(after(d1, pd), wd0, u0, g0, 0, 4, ())
         *sd, gt, gb, ut, ub = by_blocks(mine, act0, after(d1, dg), xd, sums=[*eg, *eu])
         rd = started(sd)
-        pg = by_rows(at0, after(dg, *sd), 0)
+        du, dg = dproduct(after(d1, *sd), wd0, u0, g0, 4, 4, (du, dg))
+        pg = by_rows(at0, dg, 0)
         xg = sent(pg, ACROSS)
-        pu = by_rows(at0, after(du, pg), 0)
+        pu, jr, jl = by_rows(at0, after(du, pg), 0, sums=joins(rd))
         xu = sent(pu, ACROSS)
-        *sg, jr, jl = by_rows(at0, after(dg, pu), 1, xg, sums=joins(rd))
+        ed = on(rd, jr, jl)
+        sg = by_rows(at0, after(dg, pu), 1, xg)
         rg = started(sg)
-        ed = on(rd, jr, jl)
-        su = by_rows(at0, after(du, *sg), 1, xu)
+        *su, dt, db = by_rows(at0, after(du, *sg), 1, xu, sums=ed)
         ru = started(su)
-        part = dnormed(after(dg, *su), [wg0], du, [wu0], h0, d1, 0, 6, ())
-        _, jg, ju = lax.optimization_barrier((part, joins(rg), joins(ru)))
-        sums = summed([*jg, *ju])
+        part = dnormed(after(dg, *su), [wg0], du, [wu0], h0, d1, 0, 5, ())
+        _, rg, ru = lax.optimization_barrier((part, rg, ru))
+        sums = summed([*joins(rg), *joins(ru)])
         g2, u2 = sums[:2], sums[2:]
         eg, eu = on(rg, *g2), on(ru, *u2)
-        d0, *dwd0 = dnormed(after(dg, part, *g2, *u2), [wg0], du, [wu0], h0, d1, 6, 2, (part,), sums=ed)
-        dwd = jnp.stack([jnp.concatenate(dwd0), jnp.concatenate(dwd1)])
+        d0 = dnormed(after(dg, part, *g2, *u2), [wg0], du, [wu0], h0, d1, 5, 3, (part,))
+        dwd = jnp.stack([jnp.concatenate([dt, db]), jnp.concatenate(dwd1)])
         dwg, dwu = ended([*eg, (gt,), (gb,)]), ended([*eu, (ut,), (ub,)])
         return d0[None], dwg, dwu, dwd
 

time: 1040 us -> 935 us (0.90)
  waiting for transfers between devices: 115 us -> 24.5 us
  starting transfers between devices: 37.8 us -> 25.5 us
    ppermute x42 -> x30, waiting for transfers between devices: 115 us -> 24.5 us  [sent(): return lax.ppermute(t, 'dp', pairs)]
    ppermute x42 -> x30, starting transfers between devices: 37.8 us -> 25.5 us  [sent(): return lax.ppermute(t, 'dp', pairs)]
  transfers between devices with their start and end apart: 42 -> 30, of which waited for: 9 -> 3; matrix products, arithmetic and copies ran while one was open for 0% -> 1% of each run, Pallas kernels for 34% -> 42%
where the time goes in v3:
time: 935 us; the launch traced here: 926 us
  Pallas kernels  865 us (93%)
  starting transfers between devices  25.5 us (3%)
  waiting for transfers between devices  24.5 us (3%)
    pallas_call x26, Pallas kernels, run(): made(*args, *kept, *(plane_of(t)[0] for t in added), *(u[0] for u in units))  865 us
    ppermute x30, starting transfers between devices, sent(): return lax.ppermute(t, 'dp', pairs)  25.5 us
    ppermute x30, waiting for transfers between devices, sent(): return lax.ppermute(t, 'dp', pairs)  24.5 us
  transfers between devices with their start and end apart: 30, of which 3 were waited for; matrix products, arithmetic and copies ran while one was open for 1% of the time, Pallas kernels for 42%

profile of v3, /device:TPU:0, one launch (start us, length us, event | category | flops | bytes accessed | tf_op | source)
XLA Modules:
  0.0 925.6 jit_solution(11161629518044285459)
XLA Ops:
  1.9 112.5 %shard_map.93 = (bf16[2048,1024]{1,0:T(8,128)(2,1)}, bf16[1024,2048]{1,0:T(8,128)(2,1)}, bf16[1024,6144]{1,0:T(8,128)(2,1)}, bf16[1024,6144]{1,0:T(8,128)(2,1)}) custom-call(bf16[2048,1024]{1,0:T(8,128)(2,1)} %bitcast.11, bf16[2,128,6144]{2,1,0:T(8,128)(2,1)} %refs_8_.1, bf16[2,128,6144]{2,1,0:T(8,128)(2,1)} %refs_9_.1), custom_call_target="tpu_custom_call" | custom-call | flops 16777216 | bytes 12582912 | tf_op jit(solution)/shard_map/pallas_call | solution.py:176
  114.4 103.7 %shard_map.94 = (bf16[2048,6144]{1,0:T(8,128)(2,1)}, f32[2048,6144]{1,0:T(8,128)}, f32[2048,6144]{1,0:T(8,128)}, bf16[6144,1024]{1,0:T(8,128)(2,1)}, bf16[1024,2...) custom-call(bf16[2048,1024]{1,0:T(8,128)(2,1)} %get-tuple-element.119.refs_0_, ...), custom_call_target="tpu_custom_call" | custom-call | flops 51539607552 | bytes 125829120 | tf_op jit(solution)/shard_map/pallas_call | solution.py:176
  218.1 62.4 %shard_map.95 = (bf16[2048,1024]{1,0:T(8,128)(2,1)}, bf16[2048,1024]{1,0:T(8,128)(2,1)}, bf16[1024,2048]{1,0:T(8,128)(2,1)}, bf16[6144,1024]{1,0:T(8,128)(2,1)}) custom-call(bf16[2048,6144]{1,0:T(8,128)(2,1)} %get-tuple-element.122.refs_0_.refs_1_, bf16[6144,1024]{1,0:T(8,128)(2,1)} %get-tuple-element.123.refs_1_, bf16[2048,1024]{1,0:T(8,128)(2,1)} %bitcast.12, ...), custom_call_target="tpu_custom_call" | custom-call | flops 25769803776 | bytes 25165824 | tf_op jit(solution)/shard_map/pallas_call | solution.py:176
  280.5 51.1 %shard_map.96 = (bf16[2048,6144]{1,0:T(8,128)(2,1)}, bf16[2048,6144]{1,0:T(8,128)(2,1)}, bf16[2048,6144]{1,0:T(8,128)(2,1)}, bf16[1024,2048]{1,0:T(8,128)(2,1)}, bf16[1024,2048]{1,0:T(8,128)(2,1)}) custom-call(bf16[2048,1024]{1,0:T(8,128)(2,1)} %get-tuple-element.124.refs_0_, bf16[2048,1024]{1,0:T(8,128)(2,1)} %bitcast.15, ...), custom_call_target="tpu_custom_call" | custom-call | flops 32212254720 | bytes 31457280 | tf_op jit(solution)/shard_map/pallas_call | solution.py:176
  331.6 41.3 %shard_map.97 = (bf16[2048,6144]{1,0:T(8,128)(2,1)}, bf16[2048,6144]{1,0:T(8,128)(2,1)}, bf16[2048,6144]{1,0:T(8,128)(2,1)}, bf16[1024,1536]{1,0:T(8,128)(2,1)}, bf16[1024,1536]{1,0:T(8,128)(2,1)}) custom-call(bf16[2048,1024]{1,0:T(8,128)(2,1)} %get-tuple-element.124.refs_0_, ...), custom_call_target="tpu_custom_call", output_to_operand_aliasing={{0}: (5, {}), {1}: (6, {}), {2}: (7, {})} | custom-call | flops 25769803776 | bytes 25165824 | tf_op jit(solution)/shard_map/pallas_call | solution.py:176
  372.9 27.7 %shard_map.98 = (bf16[2048,6144]{1,0:T(8,128)(2,1)}, bf16[2048,6144]{1,0:T(8,128)(2,1)}, bf16[2048,6144]{1,0:T(8,128)(2,1)}) custom-call(bf16[2048,1024]{1,0:T(8,128)(2,1)} %get-tuple-element.124.refs_0_, bf16[2048,1024]{1,0:T(8,128)(2,1)} %bitcast.17, ...), custom_call_target="tpu_custom_call", output_to_operand_aliasing={{0}: (5, {}), {1}: (6, {}), {2}: (7, {})} | custom-call | flops 19327352832 | bytes 18874368 | tf_op jit(solution)/shard_map/pallas_call | solution.py:176
  400.6 18.8 %shard_map.99 = bf16[3072,1024]{1,0:T(8,128)(2,1)} custom-call(s32[4]{0:T(128)} %get-tuple-element.234.refs_0_, bf16[2048,6144]{1,0:T(8,128)(2,1)} %get-tuple-element.141.refs_1_, bf16[2048,1024]{1,0:T(8,128)(2,1)} %bitcast.18), custom_call_target="tpu_custom_call" | custom-call | flops 12884901888 | bytes 12582912 | tf_op jit(solution)/shard_map/pallas_call | solution.py:176
  419.4 18.5 %shard_map.100 = bf16[512,6144]{1,0:T(8,128)(2,1)} custom-call(bf16[1024,2048]{1,0:T(8,128)(2,1)} %get-tuple-element.139.refs_0_, bf16[2048,6144]{1,0:T(8,128)(2,1)} %get-tuple-element.165.refs_1_.refs_0_), custom_call_target="tpu_custom_call" | custom-call | flops 12884901888 | bytes 25165824 | tf_op jit(solution)/shard_map/pallas_call | solution.py:176
  438.4 21.5 %shard_map.101 = (bf16[2,384,1024]{2,1,0:T(8,128)(2,1)}, bf16[2,384,1024]{2,1,0:T(8,128)(2,1)}, bf16[384,1024]{1,0:T(8,128)(2,1)}, bf16[384,1024]{1,0:T(8,128)(2...) custom-call(s32[4]{0:T(128)} %get-tuple-element.235.refs_0_, bf16[2048,6144]{1,0:T(8,128)(2,1)} %get-tuple-element.141.refs_1_, ...), custom_call_target="tpu_custom_call" | custom-call | flops 12884901888 | bytes 12582912 | tf_op jit(solution)/shard_map/pallas_call | solution.py:176
  459.9 18.5 %shard_map.102 = bf16[512,6144]{1,0:T(8,128)(2,1)} custom-call(bf16[1024,2048]{1,0:T(8,128)(2,1)} %get-tuple-element.139.refs_0_, bf16[2048,6144]{1,0:T(8,128)(2,1)} %get-tuple-element.158.refs_1_), custom_call_target="tpu_custom_call" | custom-call | flops 12884901888 | bytes 25165824 | tf_op jit(solution)/shard_map/pallas_call | solution.py:176
  480.5 19.2 %shard_map.103 = (bf16[2,64,6144]{2,1,0:T(8,128)(2,1)}, bf16[2,64,6144]{2,1,0:T(8,128)(2,1)}, bf16[64,6144]{1,0:T(8,128)(2,1)}, bf16[64,6144]{1,0:T(8,128)(2,1)}...) custom-call(bf16[1024,2048]{1,0:T(8,128)(2,1)} %get-tuple-element.139.refs_0_, ...), custom_call_target="tpu_custom_call" | custom-call | flops 12884901888 | bytes 25165824 | tf_op jit(solution)/shard_map/pallas_call | solution.py:176
  501.8 14.3 %collective-permute-done.3.refs_4_.refs_15_ = bf16[2,384,1024]{2,1,0:T(8,128)(2,1)} collective-permute-done((bf16[2,384,1024]{2,1,0:T(8,128)(2,1)}, bf16[2,384,1024]{2,1,0:T(8,128)(2,1)}, u32[]{:S(2)}, u32[]{:S(2)}) %collective-permute-start.3) | collective-permute-done | bytes 1572896 | tf_op jit(solution)/shard_map/ppermute | solution.py:258
  517.0 20.3 %shard_map.104 = (bf16[2,64,6144]{2,1,0:T(8,128)(2,1)}, bf16[2,64,6144]{2,1,0:T(8,128)(2,1)}, bf16[64,6144]{1,0:T(8,128)(2,1)}, bf16[64,6144]{1,0:T(8,128)(2,1)}...) custom-call(bf16[1024,2048]{1,0:T(8,128)(2,1)} %get-tuple-element.13, ...), custom_call_target="tpu_custom_call" | custom-call | flops 12884901888 | bytes 25165824 | tf_op jit(solution)/shard_map/pallas_call | solution.py:176
  550.6 66.2 %shard_map.105.refs_2_.refs_0_.refs_5_ = bf16[2048,1024]{1,0:T(8,128)(2,1)} custom-call(bf16[2048,6144]{1,0:T(8,128)(2,1)} %get-tuple-element.165.refs_1_.refs_0_, bf16[2048,6144]{1,0:T(8,128)(2,1)} %get-tuple-element.158.refs_1_, bf16[1024,2560]{1,0:T(8,128)(2,1)} %get-tuple-element.125.refs_2_, bf16[1024,2048]{1,0:T(8,128)(2,1)} %get-tuple-element.128.refs_2_.refs_3_, ...), custom_call_target="tpu_custom_call" | custom-call | flops 51539607552 | bytes 50331648 | tf_op jit(solution)/shard_map/pallas_call | solution.py:176
  616.9 21.8 %shard_map.106 = (bf16[3072,1024]{1,0:T(8,128)(2,1)}, bf16[64,6144]{1,0:T(8,128)(2,1)}, bf16[64,6144]{1,0:T(8,128)(2,1)}, bf16[64,6144]{1,0:T(8,128)(2,1)}, bf16...) custom-call(s32[4]{0:T(128)} %get-tuple-element.234.refs_0_, ...), custom_call_target="tpu_custom_call" | custom-call | flops 12884901888 | bytes 12582912 | tf_op jit(solution)/shard_map/pallas_call | solution.py:176
  642.8 34.7 %shard_map.107 = (bf16[2048,6144]{1,0:T(8,128)(2,1)}, bf16[2048,6144]{1,0:T(8,128)(2,1)}) custom-call(bf16[2048,1024]{1,0:T(8,128)(2,1)} %shard_map.105.refs_2_.refs_0_.refs_5_, bf16[6144,1024]{1,0:T(8,128)(2,1)} %get-tuple-element.123.refs_1_, f32[2048,6144]{1,0:T(8,128)} %get-tuple-element.171.refs_2_, f32[2048,6144]{1,0:T(8,128)} %get-tuple-element.172.refs_3_), custom_call_target="tpu_custom_call" | custom-call | flops 12884901888 | bytes 75497472 | tf_op jit(solution)/shard_map/pallas_call | solution.py:176
  678.7 24.3 %shard_map.108 = (bf16[2,384,1024]{2,1,0:T(8,128)(2,1)}, bf16[2,384,1024]{2,1,0:T(8,128)(2,1)}, bf16[384,1024]{1,0:T(8,128)(2,1)}, bf16[384,1024]{1,0:T(8,128)(2...) custom-call(s32[4]{0:T(128)} %get-tuple-element.235.refs_0_, ...), custom_call_target="tpu_custom_call" | custom-call | flops 12884901888 | bytes 12582912 | tf_op jit(solution)/shard_map/pallas_call | solution.py:176
  705.1 34.7 %shard_map.109 = (bf16[2048,6144]{1,0:T(8,128)(2,1)}, bf16[2048,6144]{1,0:T(8,128)(2,1)}) custom-call(bf16[2048,1024]{1,0:T(8,128)(2,1)} %shard_map.105.refs_2_.refs_0_.refs_5_, bf16[6144,1024]{1,0:T(8,128)(2,1)} %get-tuple-element.123.refs_1_, f32[2048,6144]{1,0:T(8,128)} %get-tuple-element.171.refs_2_, ...), custom_call_target="tpu_custom_call", output_to_operand_aliasing={{0}: (4, {}), {1}: (5, {})} | custom-call | flops 12884901888 | bytes 75497472 | tf_op jit(solution)/shard_map/pallas_call | solution.py:176
  739.8 18.5 %shard_map.110 = bf16[512,6144]{1,0:T(8,128)(2,1)} custom-call(bf16[1024,2048]{1,0:T(8,128)(2,1)} %get-tuple-element.188.refs_0_, bf16[2048,6144]{1,0:T(8,128)(2,1)} %get-tuple-element.221.refs_1_.refs_0_), custom_call_target="tpu_custom_call" | custom-call | flops 12884901888 | bytes 25165824 | tf_op jit(solution)/shard_map/pallas_call | solution.py:176
  759.4 19.4 %shard_map.111 = (bf16[512,6144]{1,0:T(8,128)(2,1)}, bf16[384,1024]{1,0:T(8,128)(2,1)}, bf16[384,1024]{1,0:T(8,128)(2,1)}) custom-call(bf16[1024,2048]{1,0:T(8,128)(2,1)} %get-tuple-element.188.refs_0_, bf16[2048,6144]{1,0:T(8,128)(2,1)} %get-tuple-element.199.refs_1_, bf16[384,1024]{1,0:T(8,128)(2,1)} %get-tuple-element.181.refs_2_, ...), custom_call_target="tpu_custom_call" | custom-call | flops 12884901888 | bytes 25165824 | tf_op jit(solution)/shard_map/pallas_call | solution.py:176
  782.9 19.2 %shard_map.112 = (bf16[2,64,6144]{2,1,0:T(8,128)(2,1)}, bf16[2,64,6144]{2,1,0:T(8,128)(2,1)}, bf16[64,6144]{1,0:T(8,128)(2,1)}, bf16[64,6144]{1,0:T(8,128)(2,1)}...) custom-call(bf16[1024,2048]{1,0:T(8,128)(2,1)} %get-tuple-element.188.refs_0_, ...), custom_call_target="tpu_custom_call" | custom-call | flops 12884901888 | bytes 25165824 | tf_op jit(solution)/shard_map/pallas_call | solution.py:176
  804.1 20.7 %shard_map.113 = (bf16[2,64,6144]{2,1,0:T(8,128)(2,1)}, bf16[2,64,6144]{2,1,0:T(8,128)(2,1)}, bf16[64,6144]{1,0:T(8,128)(2,1)}, bf16[64,6144]{1,0:T(8,128)(2,1)}...) custom-call(bf16[1024,2048]{1,0:T(8,128)(2,1)} %get-tuple-element.18, ...), custom_call_target="tpu_custom_call" | custom-call | flops 12884901888 | bytes 25165824 | tf_op jit(solution)/shard_map/pallas_call | solution.py:176
  826.8 44.5 %shard_map.114.refs_6_ = bf16[2048,1024]{1,0:T(8,128)(2,1)} custom-call(bf16[2048,6144]{1,0:T(8,128)(2,1)} %get-tuple-element.221.refs_1_.refs_0_, bf16[2048,6144]{1,0:T(8,128)(2,1)} %get-tuple-element.199.refs_1_, bf16[1024,6144]{1,0:T(8,128)(2,1)} %get-tuple-element.120.refs_1_.refs_2_, bf16[1024,6144]{1,0:T(8,128)(2,1)} %get-tuple-element.121.refs_2_.refs_3_, ...), custom_call_target="tpu_custom_call" | custom-call | flops 32212254720 | bytes 31457280 | tf_op jit(solution)/shard_map/pallas_call | solution.py:176
  883.9 30.1 %shard_map.116 = bf16[2048,1024]{1,0:T(8,128)(2,1)} custom-call(bf16[2048,6144]{1,0:T(8,128)(2,1)} %get-tuple-element.221.refs_1_.refs_0_, bf16[2048,6144]{1,0:T(8,128)(2,1)} %get-tuple-element.199.refs_1_, bf16[1024,6144]{1,0:T(8,128)(2,1)} %get-tuple-element.120.refs_1_.refs_2_, ...), custom_call_target="tpu_custom_call", output_to_operand_aliasing={{}: (6, {})} | custom-call | flops 19327352832 | bytes 18874368 | tf_op jit(solution)/shard_map/pallas_call | solution.py:176
  (79 shorter events, 60.7 us)
Async XLA Ops:
  437.9 42.6 %collective-permute-start.1 = (bf16[512,6144]{1,0:T(8,128)(2,1)}, bf16[512,6144]{1,0:T(8,128)(2,1)}, u32[]{:S(2)}, u32[]{:S(2)}) collective-permute-start(bf16[512,6144]{1,0:T(8,128)(2,1)} %shard_map.100), channel_id=1, source_target_pairs={{0,1},{1,0},{2,3},{3,2},{4,5},{5,4},{6,7},{7,6}} | collective-permute-start | bytes 18874376 | tf_op jit(solution)/shard_map/ppermute | solution.py:258
  478.4 38.6 %collective-permute-start.2 = (bf16[512,6144]{1,0:T(8,128)(2,1)}, bf16[512,6144]{1,0:T(8,128)(2,1)}, u32[]{:S(2)}, u32[]{:S(2)}) collective-permute-start(bf16[512,6144]{1,0:T(8,128)(2,1)} %shard_map.102), channel_id=1, source_target_pairs={{0,1},{1,0},{2,3},{3,2},{4,5},{5,4},{6,7},{7,6}} | collective-permute-start | bytes 18874376 | tf_op jit(solution)/shard_map/ppermute | solution.py:258
  478.4 37.6 %collective-permute-start.3 = (bf16[2,384,1024]{2,1,0:T(8,128)(2,1)}, bf16[2,384,1024]{2,1,0:T(8,128)(2,1)}, u32[]{:S(2)}, u32[]{:S(2)}) collective-permute-start(bf16[2,384,1024]{2,1,0:T(8,128)(2,1)} %get-tuple-element.144), channel_id=1, source_target_pairs={{0,2},{1,3},{2,6},{3,7},{4,0},{5,1},{6,4},{7,5}} | collective-permute-start | bytes 4718600 | tf_op jit(solution)/shard_map/ppermute | solution.py:258
  479.4 37.6 %collective-permute-start.4 = (bf16[2,384,1024]{2,1,0:T(8,128)(2,1)}, bf16[2,384,1024]{2,1,0:T(8,128)(2,1)}, u32[]{:S(2)}, u32[]{:S(2)}) collective-permute-start(bf16[2,384,1024]{2,1,0:T(8,128)(2,1)} %get-tuple-element.145), channel_id=1, source_target_pairs={{0,4},{1,5},{2,0},{3,1},{4,6},{5,7},{6,2},{7,3}} | collective-permute-start | bytes 4718600 | tf_op jit(solution)/shard_map/ppermute | solution.py:258
  499.7 49.9 %collective-permute-start.5 = (bf16[2,64,6144]{2,1,0:T(8,128)(2,1)}, bf16[2,64,6144]{2,1,0:T(8,128)(2,1)S(1)}, u32[]{:S(2)}, u32[]{:S(2)}) collective-permute-start(bf16[2,64,6144]{2,1,0:T(8,128)(2,1)} %get-tuple-element.152), channel_id=1, source_target_pairs={{0,2},{1,3},{2,6},{3,7},{4,0},{5,1},{6,4},{7,5}} | collective-permute-start | bytes 4718600 | tf_op jit(solution)/shard_map/ppermute | solution.py:258
  500.7 116.1 %collective-permute-start.6 = (bf16[2,64,6144]{2,1,0:T(8,128)(2,1)}, bf16[2,64,6144]{2,1,0:T(8,128)(2,1)}, u32[]{:S(2)}, u32[]{:S(2)}) collective-permute-start(bf16[2,64,6144]{2,1,0:T(8,128)(2,1)} %get-tuple-element.153), channel_id=1, source_target_pairs={{0,4},{1,5},{2,0},{3,1},{4,6},{5,7},{6,2},{7,3}} | collective-permute-start | bytes 4718600 | tf_op jit(solution)/shard_map/ppermute | solution.py:258
  537.3 79.6 %collective-permute-start.7 = (bf16[2,64,6144]{2,1,0:T(8,128)(2,1)}, bf16[2,64,6144]{2,1,0:T(8,128)(2,1)}, u32[]{:S(2)}, u32[]{:S(2)}) collective-permute-start(bf16[2,64,6144]{2,1,0:T(8,128)(2,1)} %get-tuple-element.159), channel_id=1, source_target_pairs={{0,2},{1,3},{2,6},{3,7},{4,0},{5,1},{6,4},{7,5}} | collective-permute-start | bytes 4718600 | tf_op jit(solution)/shard_map/ppermute | solution.py:258
  538.4 78.5 %collective-permute-start.8 = (bf16[2,64,6144]{2,1,0:T(8,128)(2,1)}, bf16[2,64,6144]{2,1,0:T(8,128)(2,1)}, u32[]{:S(2)}, u32[]{:S(2)}) collective-permute-start(bf16[2,64,6144]{2,1,0:T(8,128)(2,1)} %get-tuple-element.160), channel_id=1, source_target_pairs={{0,4},{1,5},{2,0},{3,1},{4,6},{5,7},{6,2},{7,3}} | collective-permute-start | bytes 4718600 | tf_op jit(solution)/shard_map/ppermute | solution.py:258
  539.3 77.5 %collective-permute-start.10 = (bf16[384,1024]{1,0:T(8,128)(2,1)}, bf16[384,1024]{1,0:T(8,128)(2,1)}, u32[]{:S(2)}, u32[]{:S(2)}) collective-permute-start(bf16[384,1024]{1,0:T(8,128)(2,1)} %get-tuple-element.168), channel_id=1, source_target_pairs={{0,4},{1,5},{2,0},{3,1},{4,6},{5,7},{6,2},{7,3}} | collective-permute-start | bytes 2359304 | tf_op jit(solution)/shard_map/ppermute | solution.py:258
  549.6 67.2 %collective-permute-start.9 = (bf16[384,1024]{1,0:T(8,128)(2,1)}, bf16[384,1024]{1,0:T(8,128)(2,1)}, u32[]{:S(2)}, u32[]{:S(2)}) collective-permute-start(bf16[384,1024]{1,0:T(8,128)(2,1)} %get-tuple-element.167), channel_id=1, source_target_pairs={{0,2},{1,3},{2,6},{3,7},{4,0},{5,1},{6,4},{7,5}} | collective-permute-start | bytes 2359304 | tf_op jit(solution)/shard_map/ppermute | solution.py:258
  638.7 38.9 %collective-permute-start.11 = (bf16[3072,1024]{1,0:T(8,128)(2,1)}, bf16[3072,1024]{1,0:T(8,128)(2,1)}, u32[]{:S(2)}, u32[]{:S(2)}) collective-permute-start(bf16[3072,1024]{1,0:T(8,128)(2,1)} %get-tuple-element.169), channel_id=1, source_target_pairs={{0,1},{1,0},{2,3},{3,2},{4,5},{5,4},{6,7},{7,6}} | collective-permute-start | bytes 18874376 | tf_op jit(solution)/shard_map/ppermute | solution.py:258
  638.7 38.8 %collective-permute-start.12 = (bf16[64,6144]{1,0:T(8,128)(2,1)}, bf16[64,6144]{1,0:T(8,128)(2,1)S(1)}, u32[]{:S(2)}, u32[]{:S(2)}) collective-permute-start(bf16[64,6144]{1,0:T(8,128)(2,1)} %get-tuple-element.175), channel_id=1, source_target_pairs={{0,2},{1,3},{2,6},{3,7},{4,0},{5,1},{6,4},{7,5}} | collective-permute-start | bytes 2359304 | tf_op jit(solution)/shard_map/ppermute | solution.py:258
  639.8 37.7 %collective-permute-start.13 = (bf16[64,6144]{1,0:T(8,128)(2,1)}, bf16[64,6144]{1,0:T(8,128)(2,1)S(1)}, u32[]{:S(2)}, u32[]{:S(2)}) collective-permute-start(bf16[64,6144]{1,0:T(8,128)(2,1)} %get-tuple-element.176), channel_id=1, source_target_pairs={{0,4},{1,5},{2,0},{3,1},{4,6},{5,7},{6,2},{7,3}} | collective-permute-start | bytes 2359304 | tf_op jit(solution)/shard_map/ppermute | solution.py:258
  640.8 36.8 %collective-permute-start.14 = (bf16[64,6144]{1,0:T(8,128)(2,1)}, bf16[64,6144]{1,0:T(8,128)(2,1)}, u32[]{:S(2)}, u32[]{:S(2)}) collective-permute-start(bf16[64,6144]{1,0:T(8,128)(2,1)} %get-tuple-element.177), channel_id=1, source_target_pairs={{0,2},{1,3},{2,6},{3,7},{4,0},{5,1},{6,4},{7,5}} | collective-permute-start | bytes 2359304 | tf_op jit(solution)/shard_map/ppermute | solution.py:258
  641.9 35.7 %collective-permute-start.15 = (bf16[64,6144]{1,0:T(8,128)(2,1)}, bf16[64,6144]{1,0:T(8,128)(2,1)}, u32[]{:S(2)}, u32[]{:S(2)}) collective-permute-start(bf16[64,6144]{1,0:T(8,128)(2,1)} %get-tuple-element.178), channel_id=1, source_target_pairs={{0,4},{1,5},{2,0},{3,1},{4,6},{5,7},{6,2},{7,3}} | collective-permute-start | bytes 2359304 | tf_op jit(solution)/shard_map/ppermute | solution.py:258
  703.1 55.2 %collective-permute-start.16 = (bf16[2,384,1024]{2,1,0:T(8,128)(2,1)}, bf16[2,384,1024]{2,1,0:T(8,128)(2,1)S(1)}, u32[]{:S(2)}, u32[]{:S(2)}) collective-permute-start(bf16[2,384,1024]{2,1,0:T(8,128)(2,1)} %get-tuple-element.179), channel_id=1, source_target_pairs={{0,2},{1,3},{2,6},{3,7},{4,0},{5,1},{6,4},{7,5}} | collective-permute-start | bytes 4718600 | tf_op jit(solution)/shard_map/ppermute | solution.py:258
  704.2 54.1 %collective-permute-start.17 = (bf16[2,384,1024]{2,1,0:T(8,128)(2,1)}, bf16[2,384,1024]{2,1,0:T(8,128)(2,1)}, u32[]{:S(2)}, u32[]{:S(2)}) collective-permute-start(bf16[2,384,1024]{2,1,0:T(8,128)(2,1)} %get-tuple-element.180), channel_id=1, source_target_pairs={{0,4},{1,5},{2,0},{3,1},{4,6},{5,7},{6,2},{7,3}} | collective-permute-start | bytes 4718600 | tf_op jit(solution)/shard_map/ppermute | solution.py:258
  802.0 72.7 %collective-permute-start.22 = (bf16[2,64,6144]{2,1,0:T(8,128)(2,1)}, bf16[2,64,6144]{2,1,0:T(8,128)(2,1)}, u32[]{:S(2)}, u32[]{:S(2)}) collective-permute-start(bf16[2,64,6144]{2,1,0:T(8,128)(2,1)} %get-tuple-element.193), channel_id=1, source_target_pairs={{0,2},{1,3},{2,6},{3,7},{4,0},{5,1},{6,4},{7,5}} | collective-permute-start | bytes 4718600 | tf_op jit(solution)/shard_map/ppermute | solution.py:258
  803.2 71.5 %collective-permute-start.23 = (bf16[2,64,6144]{2,1,0:T(8,128)(2,1)}, bf16[2,64,6144]{2,1,0:T(8,128)(2,1)}, u32[]{:S(2)}, u32[]{:S(2)}) collective-permute-start(bf16[2,64,6144]{2,1,0:T(8,128)(2,1)} %get-tuple-element.194), channel_id=1, source_target_pairs={{0,4},{1,5},{2,0},{3,1},{4,6},{5,7},{6,2},{7,3}} | collective-permute-start | bytes 4718600 | tf_op jit(solution)/shard_map/ppermute | solution.py:258
  824.8 50.0 %collective-permute-start.24 = (bf16[2,64,6144]{2,1,0:T(8,128)(2,1)}, bf16[2,64,6144]{2,1,0:T(8,128)(2,1)}, u32[]{:S(2)}, u32[]{:S(2)}) collective-permute-start(bf16[2,64,6144]{2,1,0:T(8,128)(2,1)} %get-tuple-element.202), channel_id=1, source_target_pairs={{0,2},{1,3},{2,6},{3,7},{4,0},{5,1},{6,4},{7,5}} | collective-permute-start | bytes 4718600 | tf_op jit(solution)/shard_map/ppermute | solution.py:258
  826.0 48.8 %collective-permute-start.25 = (bf16[2,64,6144]{2,1,0:T(8,128)(2,1)}, bf16[2,64,6144]{2,1,0:T(8,128)(2,1)}, u32[]{:S(2)}, u32[]{:S(2)}) collective-permute-start(bf16[2,64,6144]{2,1,0:T(8,128)(2,1)} %get-tuple-element.203), channel_id=1, source_target_pairs={{0,4},{1,5},{2,0},{3,1},{4,6},{5,7},{6,2},{7,3}} | collective-permute-start | bytes 4718600 | tf_op jit(solution)/shard_map/ppermute | solution.py:258
  879.8 34.2 %collective-permute-start.28 = (bf16[64,6144]{1,0:T(8,128)(2,1)}, bf16[64,6144]{1,0:T(8,128)(2,1)}, u32[]{:S(2)}, u32[]{:S(2)}) collective-permute-start(bf16[64,6144]{1,0:T(8,128)(2,1)} %get-tuple-element.219), channel_id=1, source_target_pairs={{0,2},{1,3},{2,6},{3,7},{4,0},{5,1},{6,4},{7,5}} | collective-permute-start | bytes 2359304 | tf_op jit(solution)/shard_map/ppermute | solution.py:258
  881.9 37.3 %collective-permute-start.26 = (bf16[64,6144]{1,0:T(8,128)(2,1)}, bf16[64,6144]{1,0:T(8,128)(2,1)S(1)}, u32[]{:S(2)}, u32[]{:S(2)}) collective-permute-start(bf16[64,6144]{1,0:T(8,128)(2,1)} %get-tuple-element.217), channel_id=1, source_target_pairs={{0,2},{1,3},{2,6},{3,7},{4,0},{5,1},{6,4},{7,5}} | collective-permute-start | bytes 2359304 | tf_op jit(solution)/shard_map/ppermute | solution.py:258
  883.0 36.1 %collective-permute-start.27 = (bf16[64,6144]{1,0:T(8,128)(2,1)}, bf16[64,6144]{1,0:T(8,128)(2,1)S(1)}, u32[]{:S(2)}, u32[]{:S(2)}) collective-permute-start(bf16[64,6144]{1,0:T(8,128)(2,1)} %get-tuple-element.218), channel_id=1, source_target_pairs={{0,4},{1,5},{2,0},{3,1},{4,6},{5,7},{6,2},{7,3}} | collective-permute-start | bytes 2359304 | tf_op jit(solution)/shard_map/ppermute | solution.py:258
  (12 other events, 219.6 us)
